TPU v7x, 32 devices: a whole 2x2x4 slice. The times are simulated.
32 devices in a mesh: frames: 16 (over z, x, core), groups: 2 (over y).
Axes of the slice: x: 2, y: 2, z: 4, core: 2. Of those that a mesh axis runs over, the one named last changes fastest.
Arguments:
- parents: bfloat16 [8, 2048, 1024], P('groups', 'frames'), may hold values from -6 to 6
- children: bfloat16 [8, 2048, 1024], P('groups', 'frames'), may hold values from -6 to 6
- child_counts: int32 [8, 16], P('groups'), may hold values from 32 to 128
- out_grad: bfloat16 [8, 2048, 1024], P('groups', 'frames'), may hold values from -6 to 6
- child_gain: bfloat16 [1024], replicated, may hold values from 0.5 to 1.5
- cross_gain: bfloat16 [1024], replicated, may hold values from 0.5 to 1.5
- cross_query: bfloat16 [1024, 1024], replicated, may hold values from -0.1875 to 0.1875
- cross_keyval: bfloat16 [1024, 2048], replicated, may hold values from -0.1875 to 0.1875
- cross_output: bfloat16 [1024, 1024], replicated, may hold values from -0.75 to 0.75
- self_gain: bfloat16 [1024], replicated, may hold values from 0.5 to 1.5
- self_project: bfloat16 [1024, 3072], replicated, may hold values from -0.1875 to 0.1875
- self_output: bfloat16 [1024, 1024], replicated, may hold values from -0.75 to 0.75
- mlp_gain: bfloat16 [1024], replicated, may hold values from 0.5 to 1.5
- mlp_up: bfloat16 [1024, 4096], replicated, may hold values from -0.1875 to 0.1875
- mlp_down: bfloat16 [4096, 1024], replicated, may hold values from -0.09375 to 0.09375
Outputs:
- top_latents: bfloat16 [8, 2048, 1024], P('groups', 'frames')
- grad_parents: float32 [8, 2048, 1024], P('groups', 'frames')
- grad_children: float32 [8, 2048, 1024], P('groups', 'frames')
- grad_child_gain: float32 [1024], P('frames')
- grad_cross_gain: float32 [1024], P('frames')
- grad_cross_query: float32 [1024, 1024], P('frames')
- grad_cross_keyval: float32 [1024, 2048], P('frames')
- grad_cross_output: float32 [1024, 1024], P('frames')
- grad_self_gain: float32 [1024], P('frames')
- grad_self_project: float32 [1024, 3072], P('frames')
- grad_self_output: float32 [1024, 1024], P('frames')
- grad_mlp_gain: float32 [1024], P('frames')
- grad_mlp_up: float32 [1024, 4096], P('frames')
- grad_mlp_down: float32 [4096, 1024], P('frames')
Inputs may be any that keep to these rules, and one draw needn't show every extreme that they name: child_counts[b, f] is the number of leading valid child latents of clip b at frame f; the rest are padding.
All inputs are finite; a program needn't handle non-finite values.
Results may differ from a plain program's by a relative error of at most 0.025.
Values may be sent and summed in bfloat16 or wider, within the bound.
A program may use at most 256 MiB of HBM per device.

v0:
```python
from functools import partial

import jax
import jax.numpy as jnp
from jax import lax
from jax.sharding import PartitionSpec as P

HEADS = 8
HEAD_DIM = 128
LEVEL = 1


def swapped(value, axis, stride):
    mask = 2**stride
    pairs = [(source, source ^ mask) for source in range(lax.axis_size(axis))]
    return lax.ppermute(value, axis, pairs)


def layer_norm(values, gain):
    average = jnp.mean(values, axis=-1, keepdims=True)
    centred = values - average
    spread = jnp.mean(centred * centred, axis=-1, keepdims=True)
    return centred * lax.rsqrt(spread + 1e-05) * gain


def norm_back(values, gain, grad_out):
    normed, pullback = jax.vjp(layer_norm, values, gain)
    return pullback(grad_out)


def matmul(left, right):
    flat = left.reshape(-1, left.shape[-1])
    result = jnp.dot(flat, right, preferred_element_type=jnp.float32)
    return result.reshape(left.shape[:-1] + (right.shape[-1],))


def backward_product(grad_rows, weight):
    flat = grad_rows.reshape(-1, grad_rows.shape[-1])
    result = lax.dot_general(
        flat, weight, (((1,), (1,)), ((), ())), preferred_element_type=jnp.float32
    )
    return result.reshape(grad_rows.shape[:-1] + (weight.shape[0],))


def weight_grad(inputs, grad_rows):
    return lax.dot_general(
        inputs.reshape(-1, inputs.shape[-1]),
        grad_rows.reshape(-1, grad_rows.shape[-1]),
        (((0,), (0,)), ((), ())),
        preferred_element_type=jnp.float32,
    )


def split_heads(rows):
    return rows.reshape(rows.shape[0], rows.shape[1], HEADS, HEAD_DIM)


def attend_scores(queries, key_rows, key_valid):
    scores = jnp.einsum(
        "cqhd,ckhd->chqk",
        split_heads(queries),
        split_heads(key_rows),
        preferred_element_type=jnp.float32,
    ) * HEAD_DIM ** (-0.5)
    return jnp.where(key_valid[:, None, None, :], scores, -1e30)


def attend_forward(queries, key_rows, value_rows, key_valid):
    scores = attend_scores(queries, key_rows, key_valid)
    top_score = jnp.max(scores, axis=-1, keepdims=True)
    log_total = top_score + jnp.log(jnp.sum(jnp.exp(scores - top_score), axis=-1, keepdims=True))
    weights = jnp.exp(scores - log_total).astype(jnp.bfloat16)
    mixture = jnp.einsum(
        "chqk,ckhd->cqhd", weights, split_heads(value_rows), preferred_element_type=jnp.float32
    )
    return (mixture.reshape(queries.shape), log_total)


def attend_backward(queries, key_rows, value_rows, key_valid, log_total, grad_mix):
    scores = attend_scores(queries, key_rows, key_valid)
    attention = jnp.exp(scores - log_total)
    grad_heads = split_heads(grad_mix)
    grad_weights = jnp.einsum(
        "cqhd,ckhd->chqk", grad_heads, split_heads(value_rows), preferred_element_type=jnp.float32
    )
    inner_sum = jnp.sum(attention * grad_weights, axis=-1, keepdims=True)
    grad_scores = (attention * (grad_weights - inner_sum)).astype(jnp.bfloat16)
    scaling = HEAD_DIM ** (-0.5)
    grad_query = (
        jnp.einsum(
            "chqk,ckhd->cqhd",
            grad_scores,
            split_heads(key_rows),
            preferred_element_type=jnp.float32,
        )
        * scaling
    )
    grad_key = (
        jnp.einsum(
            "chqk,cqhd->ckhd", grad_scores, split_heads(queries), preferred_element_type=jnp.float32
        )
        * scaling
    )
    grad_value = jnp.einsum(
        "chqk,cqhd->ckhd",
        attention.astype(jnp.bfloat16),
        grad_heads,
        preferred_element_type=jnp.float32,
    )
    return (
        grad_query.reshape(queries.shape),
        grad_key.reshape(key_rows.shape),
        grad_value.reshape(value_rows.shape),
    )


def body(
    parents,
    children,
    child_counts,
    out_grad,
    child_gain,
    cross_gain,
    cross_query,
    cross_keyval,
    cross_output,
    self_gain,
    self_project,
    self_output,
    mlp_gain,
    mlp_up,
    mlp_down,
):
    features = parents.shape[2]
    half_rows = parents.shape[1]
    child_size = children.shape[1]
    frame_index = lax.axis_index("frames")
    partner_index = jnp.bitwise_xor(frame_index, 1 << LEVEL)
    frame_ids = jnp.arange(child_counts.shape[1], dtype=jnp.int32)
    own_count = jnp.sum(jnp.where(frame_ids[None, :] == frame_index, child_counts, 0), axis=1)
    partner_count = jnp.sum(jnp.where(frame_ids[None, :] == partner_index, child_counts, 0), axis=1)
    positions = jnp.arange(child_size, dtype=jnp.int32)
    child_valid = jnp.concatenate(
        [positions[None, :] < own_count[:, None], positions[None, :] < partner_count[:, None]],
        axis=1,
    )
    node_valid = jnp.ones((parents.shape[0], 2 * half_rows), jnp.int32) > 0
    gain_child = child_gain.astype(jnp.float32)
    gain_cross = cross_gain.astype(jnp.float32)
    gain_self = self_gain.astype(jnp.float32)
    gain_mlp = mlp_gain.astype(jnp.float32)
    latents = parents.astype(jnp.float32)
    child_latents = children.astype(jnp.float32)
    child_in = layer_norm(child_latents, gain_child).astype(jnp.bfloat16)
    keyval = matmul(child_in, cross_keyval).astype(jnp.bfloat16)
    partner_keyval = swapped(keyval, "frames", LEVEL)
    cross_keys = jnp.concatenate([keyval, partner_keyval], axis=1)
    cross_in = layer_norm(latents, gain_cross).astype(jnp.bfloat16)
    cross_queries = matmul(cross_in, cross_query).astype(jnp.bfloat16)
    cross_mix, cross_total = attend_forward(
        cross_queries, cross_keys[..., :features], cross_keys[..., features:], child_valid
    )
    cross_mixed = cross_mix.astype(jnp.bfloat16)
    after_cross = latents + matmul(cross_mixed, cross_output)
    self_in = layer_norm(after_cross, gain_self).astype(jnp.bfloat16)
    projected = matmul(self_in, self_project).astype(jnp.bfloat16)
    partner_self = swapped(projected[..., features:], "frames", LEVEL)
    self_keys = jnp.concatenate([projected[..., features:], partner_self], axis=1)
    self_mix, self_total = attend_forward(
        projected[..., :features], self_keys[..., :features], self_keys[..., features:], node_valid
    )
    self_mixed = self_mix.astype(jnp.bfloat16)
    after_self = after_cross + matmul(self_mixed, self_output)
    mlp_in = layer_norm(after_self, gain_mlp).astype(jnp.bfloat16)
    hidden = matmul(mlp_in, mlp_up)
    activated, gelu_back = jax.vjp(partial(jax.nn.gelu, approximate=False), hidden)
    activated_low = activated.astype(jnp.bfloat16)
    top_latents = (after_self + matmul(activated_low, mlp_down)).astype(jnp.bfloat16)
    grad_top = out_grad.astype(jnp.float32)
    grad_low = grad_top.astype(jnp.bfloat16)
    grad_down = weight_grad(activated_low, grad_low)
    grad_hidden = gelu_back(backward_product(grad_low, mlp_down))[0].astype(jnp.bfloat16)
    grad_up = weight_grad(mlp_in, grad_hidden)
    grad_norm_mlp, grad_gain_mlp = norm_back(
        after_self, gain_mlp, backward_product(grad_hidden, mlp_up)
    )
    grad_after_self = grad_top + grad_norm_mlp
    grad_self_out = grad_after_self.astype(jnp.bfloat16)
    grad_self_weight = weight_grad(self_mixed, grad_self_out)
    grad_self_mix = backward_product(grad_self_out, self_output).astype(jnp.bfloat16)
    again_in = layer_norm(after_cross, gain_self).astype(jnp.bfloat16)
    again_project = matmul(again_in, self_project).astype(jnp.bfloat16)
    again_partner = swapped(again_project[..., features:], "frames", LEVEL)
    used_keys = jnp.concatenate([again_project[..., features:], again_partner], axis=1)
    grad_self_query, grad_self_key, grad_self_value = attend_backward(
        again_project[..., :features],
        used_keys[..., :features],
        used_keys[..., features:],
        node_valid,
        self_total,
        grad_self_mix,
    )
    self_returned = swapped(
        jnp.concatenate([grad_self_key[:, half_rows:], grad_self_value[:, half_rows:]], axis=-1),
        "frames",
        LEVEL,
    )
    own_self_kv = jnp.concatenate(
        [grad_self_key[:, :half_rows], grad_self_value[:, :half_rows]], axis=-1
    )
    grad_projected = jnp.concatenate(
        [grad_self_query, own_self_kv + self_returned], axis=-1
    ).astype(jnp.bfloat16)
    grad_project = weight_grad(again_in, grad_projected)
    grad_norm_self, grad_gain_self = norm_back(
        after_cross, gain_self, backward_product(grad_projected, self_project)
    )
    grad_after_cross = grad_after_self + grad_norm_self
    grad_cross_out = grad_after_cross.astype(jnp.bfloat16)
    grad_cross_weight = weight_grad(cross_mixed, grad_cross_out)
    grad_cross_mix = backward_product(grad_cross_out, cross_output).astype(jnp.bfloat16)
    grad_cross_q, grad_cross_k, grad_cross_v = attend_backward(
        cross_queries,
        cross_keys[..., :features],
        cross_keys[..., features:],
        child_valid,
        cross_total,
        grad_cross_mix,
    )
    child_returned = swapped(
        jnp.concatenate([grad_cross_k[:, child_size:], grad_cross_v[:, child_size:]], axis=-1),
        "frames",
        LEVEL,
    )
    own_child_kv = jnp.concatenate(
        [grad_cross_k[:, :child_size], grad_cross_v[:, :child_size]], axis=-1
    )
    grad_keyval = (own_child_kv + child_returned).astype(jnp.bfloat16)
    grad_query_low = grad_cross_q.astype(jnp.bfloat16)
    grad_query_weight = weight_grad(cross_in, grad_query_low)
    grad_norm_cross, grad_gain_cross = norm_back(
        latents, gain_cross, backward_product(grad_query_low, cross_query)
    )
    grad_parents = grad_after_cross + grad_norm_cross
    grad_keyval_weight = weight_grad(child_in, grad_keyval)
    grad_children, grad_gain_child = norm_back(
        child_latents, gain_child, backward_product(grad_keyval, cross_keyval)
    )
    shares = (
        lax.psum_scatter(
            grad_gain_child.astype(jnp.bfloat16), "frames", scatter_dimension=0, tiled=True
        ).astype(jnp.float32),
        lax.psum_scatter(
            grad_gain_cross.astype(jnp.bfloat16), "frames", scatter_dimension=0, tiled=True
        ).astype(jnp.float32),
        lax.psum_scatter(
            grad_query_weight.astype(jnp.bfloat16), "frames", scatter_dimension=0, tiled=True
        ).astype(jnp.float32),
        lax.psum_scatter(
            grad_keyval_weight.astype(jnp.bfloat16), "frames", scatter_dimension=0, tiled=True
        ).astype(jnp.float32),
        lax.psum_scatter(
            grad_cross_weight.astype(jnp.bfloat16), "frames", scatter_dimension=0, tiled=True
        ).astype(jnp.float32),
        lax.psum_scatter(
            grad_gain_self.astype(jnp.bfloat16), "frames", scatter_dimension=0, tiled=True
        ).astype(jnp.float32),
        lax.psum_scatter(
            grad_project.astype(jnp.bfloat16), "frames", scatter_dimension=0, tiled=True
        ).astype(jnp.float32),
        lax.psum_scatter(
            grad_self_weight.astype(jnp.bfloat16), "frames", scatter_dimension=0, tiled=True
        ).astype(jnp.float32),
        lax.psum_scatter(
            grad_gain_mlp.astype(jnp.bfloat16), "frames", scatter_dimension=0, tiled=True
        ).astype(jnp.float32),
        lax.psum_scatter(
            grad_up.astype(jnp.bfloat16), "frames", scatter_dimension=0, tiled=True
        ).astype(jnp.float32),
        lax.psum_scatter(
            grad_down.astype(jnp.bfloat16), "frames", scatter_dimension=0, tiled=True
        ).astype(jnp.float32),
    )
    totals = lax.psum(
        (
            shares[0],
            shares[1],
            shares[2],
            shares[3],
            shares[4],
            shares[5],
            shares[6],
            shares[7],
            shares[8],
            shares[9],
            shares[10],
        ),
        "groups",
    )
    return (
        top_latents,
        grad_parents,
        grad_children,
        totals[0],
        totals[1],
        totals[2],
        totals[3],
        totals[4],
        totals[5],
        totals[6],
        totals[7],
        totals[8],
        totals[9],
        totals[10],
    )


def solution(mesh):
    return jax.shard_map(
        body,
        mesh=mesh,
        in_specs=(
            P("groups", "frames", None),
            P("groups", "frames", None),
            P("groups", None),
            P("groups", "frames", None),
            P(),
            P(),
            P(),
            P(),
            P(),
            P(),
            P(),
            P(),
            P(),
            P(),
            P(),
        ),
        out_specs=(
            P("groups", "frames", None),
            P("groups", "frames", None),
            P("groups", "frames", None),
            P("frames"),
            P("frames"),
            P("frames", None),
            P("frames", None),
            P("frames", None),
            P("frames"),
            P("frames", None),
            P("frames", None),
            P("frames"),
            P("frames", None),
            P("frames", None),
        ),
        check_vma=False,
    )
```

profile of v0, /device:TPU:0, one launch (start us, length us, event | category | flops | bytes accessed | tf_op | source)
XLA Modules:
  0.0 972.9 jit_solution(2113327104153718728)
XLA Ops:
  11.2 6.1 fusion.34
  17.2 3.0 collective-permute-start
  20.9 2.3 fusion.92
  23.3 2.4 copy.114
  26.0 40.3 %collective-permute-done = bf16[4,128,2048]{2,1,0:T(8,128)(2,1)} collective-permute-done((bf16[4,128,2048]{2,1,0:T(8,128)(2,1)}, bf16[4,128,2048]{2,1,0:T(8,128)(2,1)}, u32[]{:S(2)}, u32[]{:S(2)}) %collective-permute-start) | collective-permute-done | bytes 2097184 | tf_op jit(solution)/shard_map/ppermute | solution.py:16
  66.2 3.8 pad_maximum_fusion.4
  70.0 3.9 copy.115
  73.9 3.2 fusion.29
  83.9 4.0 fusion.20
  89.5 1.7 collective-permute-start.1
  92.3 2.3 copy.116
  94.5 42.1 %collective-permute-done.1 = bf16[4,128,2048]{2,1,0:T(8,128)(2,1)} collective-permute-done((bf16[4,128,2048]{2,1,0:T(8,128)(2,1)}, bf16[4,128,2048]{2,1,0:T(8,128)(2,1)}, u32[]{:S(2)}, u32[]{:S(2)}) %collective-permute-start.1) | collective-permute-done | bytes 2097184 | tf_op jit(solution)/shard_map/ppermute | solution.py:16
  136.6 3.8 pad_maximum_fusion.3
  140.3 3.9 copy.117
  144.3 2.9 multiply_reduce_fusion.2
  153.7 9.8 %fusion.80 = (u8[128,4096]{1,0:T(8,128)(4,1)S(1)}, u8[128,4096]{1,0:T(8,128)(4,1)S(1)}, f32[4,128,4096]{2,1,0:T(8,128)S(1)}) fusion(bf16[1024,4096]{1,0:T(8,128)(2,1)} %param.28, f32[4,128,1024]{2,1,0:T(8,128)S(1)} %get-tuple-element.64, f32[1024]{0:T(1024)S(1)} %convert_element_type.204, f32[4,128]{1,0:T(4,128)S(1)} %fusion.126, ...), kind=kOutput, calls=%fused_computation.142 | convolution fusion | flops 4323278848 | bytes 19931136 | tf_op jit(solution)/shard_map/dot_general | solution.py:33
  163.5 19.9 %multiply_convert_fusion = (bf16[4,128,4096]{2,1,0:T(8,128)(2,1)}, f32[4,128,4096]{2,1,0:T(8,128)}) fusion(f32[4,128,4096]{2,1,0:T(8,128)S(1)} %get-tuple-element.65, u8[128,4096]{1,0:T(8,128)(4,1)S(1)} %get-tuple-element.15, u8[128,4096]{1,0:T(8,128)(4,1)S(1)} %get-tuple-element.14), kind=kLoop, calls=%fused_computation.20 | loop fusion | flops 146800640 | bytes 22020096 | tf_op jit(solution)/shard_map/convert_element_type | solution.py:177
  183.4 13.1 %add_convert_fusion = bf16[4,128,4096]{2,1,0:T(8,128)(2,1)S(1)} fusion(f32[4,128,4096]{2,1,0:T(8,128)} %get-tuple-element.44, f32[4,128,4096]{2,1,0:T(8,128)} %copy-done.27, bf16[4,128,1024]{2,1,0:T(8,128)(2,1)S(1)} %copy-done.36, bf16[4096,1024]{1,0:T(8,128)(2,1)} %param.29), kind=kOutput, calls=%fused_computation.19 | convolution fusion | flops 4324327424 | bytes 30408704 | tf_op jit(solution)/shard_map/dot_general | solution.py:39
  196.5 9.3 multiply_reduce_fusion.3
  208.8 2.3 fusion.98
  211.1 2.4 copy.118
  213.5 4.6 multiply_reduce_fusion.1
  218.2 2.6 fusion.117
  222.7 2.3 fusion.139
  225.0 2.9 copy.108
  227.9 4.5 fusion.140
  232.4 2.9 copy.109
  235.3 4.8 pad_maximum_fusion
  243.3 2.4 copy.80
  245.7 1.8 copy.106
  247.5 3.1 copy.107
  250.6 2.6 bitcast_convert_fusion.4
  253.3 85.1 %collective-permute-done.2 = f32[4,128,2048]{2,1,0:T(8,128)} collective-permute-done((f32[4,128,2048]{2,1,0:T(8,128)}, f32[4,128,2048]{2,1,0:T(8,128)}, u32[]{:S(2)}, u32[]{:S(2)}) %collective-permute-start.2) | collective-permute-done | bytes 4194336 | tf_op jit(solution)/shard_map/ppermute | solution.py:16
  338.4 4.1 fusion.23
  342.5 6.5 multiply_reduce_fusion.5
  353.1 2.6 bitcast_convert_fusion.5
  355.7 4.5 fusion.95
  360.2 2.3 copy.119
  362.5 5.5 multiply_reduce_fusion
  371.9 2.9 bitcast_convert_fusion.6
  375.3 10.8 %bitcast_convert_fusion.1 = bf16[1024,4096]{1,0:T(8,128)(2,1)} fusion(bf16[4,128,4096]{2,1,0:T(8,128)(2,1)} %copy-done.67, f32[4,128,1024]{2,1,0:T(8,128)} %copy-done.10, f32[1024]{0:T(1024)S(1)} %convert_element_type.204, f32[4,128]{1,0:T(4,128)S(1)} %fusion.126, f32[4,128]{1,0:T(4,128)S(1)} %broadcast_multiply_fusion), kind=kOutput, calls=%fused_computation.1 | convolution fusion | flops 4301258752 | bytes 14688256 | tf_op jit(solution)/shard_map/dot_general | solution.py:46
  386.1 10.3 %bitcast_convert_fusion = bf16[4096,1024]{1,0:T(8,128)(2,1)} fusion(bf16[4,128,4096]{2,1,0:T(8,128)(2,1)} %get-tuple-element.43, bf16[4,128,1024]{2,1,0:T(8,128)(2,1)} %param.18), kind=kOutput, calls=%fused_computation | convolution fusion | flops 4299161600 | bytes 13631488 | tf_op jit(solution)/shard_map/dot_general | solution.py:46
  396.5 7.5 bitcast_convert_fusion.2
  405.3 2.9 fusion.120
  408.2 2.3 fusion.138
  410.5 3.1 copy.113
  413.6 1.9 convolution_multiply_fusion
  417.1 1.8 copy.112
  418.9 4.9 pad_maximum_fusion.1
  425.1 1.8 copy.111
  426.9 3.1 copy.110
  430.0 91.5 %collective-permute-done.3 = f32[4,128,2048]{2,1,0:T(8,128)} collective-permute-done((f32[4,128,2048]{2,1,0:T(8,128)}, f32[4,128,2048]{2,1,0:T(8,128)}, u32[]{:S(2)}, u32[]{:S(2)}) %collective-permute-start.3) | collective-permute-done | bytes 4194336 | tf_op jit(solution)/shard_map/ppermute | solution.py:16
  521.5 4.8 fusion.24
  527.6 4.6 bitcast_convert_fusion.3
  534.2 10.2 %add_convert_fusion.1 = bf16[4,128,1024]{2,1,0:T(8,128)(2,1)} fusion(f32[4,128,1024]{2,1,0:T(8,128)S(1)} %copy-done.11, bf16[4,128,4096]{2,1,0:T(8,128)(2,1)} %get-tuple-element.43, bf16[4096,1024]{1,0:T(8,128)(2,1)} %param.29), kind=kOutput, calls=%fused_computation.136 | convolution fusion | flops 4296015872 | bytes 15728640 | tf_op jit(solution)/shard_map/dot_general | solution.py:33
  544.4 3.6 fusion.54
  549.6 2.0 add_add_fusion.4
  551.7 5.4 fusion.52
  558.4 30.5 %all-reduce.5 = (bf16[1024]{0:T(1024)(128)(2,1)S(1)}, bf16[1024]{0:T(1024)(128)(2,1)S(1)}, bf16[1024]{0:T(1024)(128)(2,1)S(1)}, bf16[1024]{0:T(1024)(128)(2,1)S(1)}) all-reduce(bf16[1024]{0:T(1024)(128)(2,1)S(1)} %get-tuple-element.22, ...), channel_id=2, replica_groups=mesh['frames'=16,'groups'=2] {'frames'}, use_global_device_ids=true, to_apply=%region_25.26.clone | all-reduce | flops 4096 | bytes 16384
  591.3 3.7 broadcast_add_fusion
  596.3 107.2 %reduce-scatter.20.cloned.1.call-done = bf16[256,1024]{1,0:T(8,128)(2,1)} async-done(((bf16[4096,1024]{1,0:T(8,128)(2,1)}), bf16[256,1024]{1,0:T(8,128)(2,1)}) %reduce-scatter.20.cloned.1.call-update) | async-done | bytes 524304 | tf_op jit(solution)/shard_map/reduce_scatter | solution.py:280
  703.5 88.6 %reduce-scatter.14.cloned.1.call-done = bf16[64,3072]{1,0:T(8,128)(2,1)} async-done(((bf16[1024,3072]{1,0:T(8,128)(2,1)}), bf16[64,3072]{1,0:T(8,128)(2,1)}) %reduce-scatter.14.cloned.1.call-update) | async-done | bytes 393232 | tf_op jit(solution)/shard_map/reduce_scatter | solution.py:268
  792.0 75.7 %reduce-scatter.10.cloned.1.call-done = bf16[64,2048]{1,0:T(8,128)(2,1)} async-done(((bf16[1024,2048]{1,0:T(8,128)(2,1)}), bf16[64,2048]{1,0:T(8,128)(2,1)}) %reduce-scatter.10.cloned.1.call-update) | async-done | bytes 262160 | tf_op jit(solution)/shard_map/reduce_scatter | solution.py:259
  867.7 98.1 %all-reduce.7 = (f32[64]{0:T(128)}, f32[64]{0:T(128)}, f32[64,1024]{1,0:T(8,128)}, f32[64,2048]{1,0:T(8,128)}, f32[64,1024]{1,0:T(8,128)}, /*index=5*/f32[64]{0:...) all-reduce(f32[64]{0:T(128)} %dynamic-slice_convert_fusion.3, ...), channel_id=1, replica_groups=mesh['frames'=16,'groups'=2] {'groups'}, use_global_device_ids=true, to_apply=%region_26.27 | all-reduce | flops 1048832 | bytes 6293504 | tf_op jit(solution)/shard_map/psum | solution.py:284
  (219 shorter events, 50.5 us)
Async XLA Ops:
  7.2 144.7 %copy-start = (bf16[1024,1024]{1,0:T(8,128)(2,1)S(1)}, bf16[1024,1024]{1,0:T(8,128)(2,1)}, u32[]{:S(2)}) copy-start(bf16[1024,1024]{1,0:T(8,128)(2,1)} %param.26) | copy-start | bytes 6291460
  7.2 3.9 copy-start.60
  7.2 537.2 %reduce-scatter.16.cloned.1.call-start = ((), (), s32[]{:S(2)}) async-start(), calls=%async_computation.11 | async-start | bytes 2228224 | tf_op jit(solution)/shard_map/reduce_scatter | solution.py:271
  7.3 3.9 copy-start.20
  8.9 8.4 copy-start.52
  11.1 6.1 copy-start.58
  11.1 6.1 copy-start.50
  11.1 9.1 copy-start.61
  11.1 9.1 copy-start.9
  17.2 3.7 copy-start.65
  17.2 49.0 %collective-permute-start = (bf16[4,128,2048]{2,1,0:T(8,128)(2,1)}, bf16[4,128,2048]{2,1,0:T(8,128)(2,1)}, u32[]{:S(2)}, u32[]{:S(2)}) collective-permute-start(bf16[4,128,2048]{2,1,0:T(8,128)(2,1)} %fusion.34), channel_id=1, source_target_pairs={{0,4},{2,6},{4,0},{6,2},{8,12},{10,14},{12,8},{14,10},{16,20},{18,... | collective-permute-start | bytes 6291464 | tf_op jit(solution)/shard_map/ppermute | solution.py:16
  20.9 2.3 copy-start.56
  23.2 2.4 copy-start.62
  23.2 2.5 copy-start.64
  77.1 2.1 copy-start.4
  77.1 3.1 copy-start.31
  77.1 6.8 slice-start
  80.2 1.9 copy-start.40
  80.2 3.7 slice-start.1
  83.5 4.4 copy-start.6
  87.9 3.3 copy-start.63
  89.5 47.1 %collective-permute-start.1 = (bf16[4,128,2048]{2,1,0:T(8,128)(2,1)}, bf16[4,128,2048]{2,1,0:T(8,128)(2,1)}, u32[]{:S(2)}, u32[]{:S(2)}) collective-permute-start(bf16[4,128,2048]{2,1,0:T(8,128)(2,1)} %slice.66), channel_id=1, source_target_pairs={{0,4},{2,6},{4,0},{6,2},{8,12},{10,14},{12,8},{14,10},{16,20},{18,... | collective-permute-start | bytes 6291464 | tf_op jit(solution)/shard_map/ppermute | solution.py:16
  147.1 2.1 copy-start.2
  147.1 3.1 copy-start.18
  153.3 52.5 %copy-start.10 = (f32[4,128,1024]{2,1,0:T(8,128)}, f32[4,128,1024]{2,1,0:T(8,128)S(1)}, u32[]{:S(2)}) copy-start(f32[4,128,1024]{2,1,0:T(8,128)S(1)} %get-tuple-element.64) | copy-start | bytes 6291460
  163.5 19.9 %copy-start.27 = (f32[4,128,4096]{2,1,0:T(8,128)}, f32[4,128,4096]{2,1,0:T(8,128)S(1)}, u32[]{:S(2)}) copy-start(f32[4,128,4096]{2,1,0:T(8,128)S(1)} %get-tuple-element.65) | copy-start | bytes 25165828
  163.5 19.9 %copy-start.36 = (bf16[4,128,1024]{2,1,0:T(8,128)(2,1)S(1)}, bf16[4,128,1024]{2,1,0:T(8,128)(2,1)}, u32[]{:S(2)}) copy-start(bf16[4,128,1024]{2,1,0:T(8,128)(2,1)} %param.18) | copy-start | bytes 3145732
  196.5 9.3 copy-start.67
  211.1 2.4 copy-start.19
  213.5 4.6 copy-start.3
  213.5 4.6 copy-start.26
  235.3 6.3 copy-start.14
  240.1 98.2 %collective-permute-start.2 = (f32[4,128,2048]{2,1,0:T(8,128)}, f32[4,128,2048]{2,1,0:T(8,128)}, u32[]{:S(2)}, u32[]{:S(2)}) collective-permute-start(f32[4,128,2048]{2,1,0:T(8,128)} %pad_maximum_fusion), channel_id=1, source_target_pairs={{0,4},{2,6},{4,0},{6,2},{8,12},{10,14},{12,8},{14,10},{16,20},{18,... | collective-permute-start | bytes 12582920 | tf_op jit(solution)/shard_map/ppermute | solution.py:16
  243.3 2.4 copy-start.29
  247.5 3.1 copy-start.35
  247.5 3.1 copy-start.46
  253.2 89.3 %copy-start.8 = (f32[4,128,1024]{2,1,0:T(8,128)S(1)}, f32[4,128,1024]{2,1,0:T(8,128)}, u32[]{:S(2)}) copy-start(f32[4,128,1024]{2,1,0:T(8,128)} %copy-done.6) | copy-start | bytes 6291460
  253.2 298.4 %reduce-scatter.12.cloned.1.call-start = ((), (), s32[]{:S(2)}) async-start(), calls=%async_computation.9 | async-start | bytes 2228224 | tf_op jit(solution)/shard_map/reduce_scatter | solution.py:262
  253.3 89.2 %copy-start.42 = (bf16[4,128,1024]{2,1,0:T(8,128)(2,1)S(1)}, bf16[4,128,1024]{2,1,0:T(8,128)(2,1)}, u32[]{:S(2)}) copy-start(bf16[4,128,1024]{2,1,0:T(8,128)(2,1)} %copy.80) | copy-start | bytes 3145732
  342.5 6.5 copy-start.38
  349.0 1.8 copy-start.37
  350.9 2.2 copy-start.44
  355.7 196.0 %reduce-scatter.8.cloned.1.call-start = ((), (), s32[]{:S(2)}) async-start(), calls=%async_computation.7 | async-start | bytes 2228224 | tf_op jit(solution)/shard_map/reduce_scatter | solution.py:256
  362.5 5.5 copy-start.5
  374.8 221.5 %reduce-scatter.18.cloned.1.call-start = ((), (), s32[]{:S(2)}) async-start(), calls=%async_computation.12 | async-start | bytes 8912896 | tf_op jit(solution)/shard_map/reduce_scatter | solution.py:277
  386.1 317.4 %reduce-scatter.20.cloned.1.call-start = ((), (), s32[]{:S(2)}) async-start(), calls=%async_computation.13 | async-start | bytes 8912896 | tf_op jit(solution)/shard_map/reduce_scatter | solution.py:280
  396.4 395.6 %reduce-scatter.14.cloned.1.call-start = ((), (), s32[]{:S(2)}) async-start(), calls=%async_computation.10 | async-start | bytes 6684672 | tf_op jit(solution)/shard_map/reduce_scatter | solution.py:268
  404.1 463.7 %reduce-scatter.10.cloned.1.call-start = ((), (), s32[]{:S(2)}) async-start(), calls=%async_computation.8 | async-start | bytes 4456448 | tf_op jit(solution)/shard_map/reduce_scatter | solution.py:259
  410.5 3.1 copy-start.13
  418.9 6.1 copy-start.30
  423.9 97.6 %collective-permute-start.3 = (f32[4,128,2048]{2,1,0:T(8,128)}, f32[4,128,2048]{2,1,0:T(8,128)}, u32[]{:S(2)}, u32[]{:S(2)}) collective-permute-start(f32[4,128,2048]{2,1,0:T(8,128)} %pad_maximum_fusion.1), channel_id=1, source_target_pairs={{0,4},{2,6},{4,0},{6,2},{8,12},{10,14},{12,8},{14,10},{16,20},{18,... | collective-permute-start | bytes 12582920 | tf_op jit(solution)/shard_map/ppermute | solution.py:16
  430.0 97.7 %copy-start.21 = (bf16[4,128,1024]{2,1,0:T(8,128)(2,1)S(1)}, bf16[4,128,1024]{2,1,0:T(8,128)(2,1)}, u32[]{:S(2)}) copy-start(bf16[4,128,1024]{2,1,0:T(8,128)(2,1)} %param.16) | copy-start | bytes 3145732
  430.0 97.7 %copy-start.51 = (f32[1024]{0:T(1024)S(1)}, f32[1024]{0:T(1024)}, u32[]{:S(2)}) copy-start(f32[1024]{0:T(1024)} %copy-done.50) | copy-start | bytes 12292
  430.0 97.6 %copy-start.53 = (f32[4,128]{1,0:T(4,128)S(1)}, f32[4,128]{1,0:T(4,128)}, u32[]{:S(2)}) copy-start(f32[4,128]{1,0:T(4,128)} %copy-done.52) | copy-start | bytes 6148
  430.0 97.6 %copy-start.59 = (f32[4,128]{1,0:T(4,128)S(1)}, f32[4,128]{1,0:T(4,128)}, u32[]{:S(2)}) copy-start(f32[4,128]{1,0:T(4,128)} %copy-done.58) | copy-start | bytes 6148
  532.3 1.9 copy-start.11
  544.4 3.7 copy-start.57
  549.6 2.0 copy-start.22
  551.7 5.4 copy-start.55
  557.1 34.2 %copy-start.23 = (bf16[4,128,1024]{2,1,0:T(8,128)(2,1)S(1)}, bf16[4,128,1024]{2,1,0:T(8,128)(2,1)}, u32[]{:S(2)}) copy-start(bf16[4,128,1024]{2,1,0:T(8,128)(2,1)} %param.16) | copy-start | bytes 3145732
  591.2 276.5 %copy-start.47 = (bf16[64,1024]{1,0:T(8,128)(2,1)S(1)}, bf16[64,1024]{1,0:T(8,128)(2,1)}, u32[]{:S(2)}) copy-start(bf16[64,1024]{1,0:T(8,128)(2,1)} %reduce-scatter.16.cloned.1.call-done) | copy-start | bytes 393220
  591.2 276.5 %copy-start.48 = (bf16[64,1024]{1,0:T(8,128)(2,1)S(1)}, bf16[64,1024]{1,0:T(8,128)(2,1)}, u32[]{:S(2)}) copy-start(bf16[64,1024]{1,0:T(8,128)(2,1)} %reduce-scatter.12.cloned.1.call-done) | copy-start | bytes 393220
  591.2 276.5 %copy-start.49 = (bf16[64,1024]{1,0:T(8,128)(2,1)S(1)}, bf16[64,1024]{1,0:T(8,128)(2,1)}, u32[]{:S(2)}) copy-start(bf16[64,1024]{1,0:T(8,128)(2,1)} %reduce-scatter.8.cloned.1.call-done) | copy-start | bytes 393220
  591.3 374.6 %copy-start.1 = (bf16[1024,1024]{1,0:T(8,128)(2,1)S(1)}, bf16[1024,1024]{1,0:T(8,128)(2,1)}, u32[]{:S(2)}) copy-start(bf16[1024,1024]{1,0:T(8,128)(2,1)} %param.26) | copy-start | bytes 6291460
  (17 other events, 21.9 us)
Sparse Core Ops, SparseCore 0:
  253.3 68.7 reduce-scatter.15
  355.8 62.6 reduce-scatter.11
  422.3 67.2 reduce-scatter.7
  493.5 102.7 reduce-scatter.17
  600.2 103.2 reduce-scatter.19
  707.2 84.7 reduce-scatter.13
  795.9 71.8 reduce-scatter.9
where the time goes:
time: 977 us; the launch traced here: 973 us
  waiting for transfers between devices  532 us (54%)
  matrix products  151 us (15%)
  blocking collectives  129 us (13%)
  other arithmetic  69.3 us (7%)
  local copies, waits for them, and re-layouts  68.4 us (7%)
  between operations  15.9 us (2%)
    ppermute x4, waiting for transfers between devices, swapped(): return lax.ppermute(value, axis, pairs)  259 us
    reduce_scatter x1, waiting for transfers between devices, body(): lax.psum_scatter(grad_down.astype(jnp.bfloat16), 'frames', scatter_dimens...  107 us
    psum x1, blocking collectives, body(): lax.psum((shares[0], shares[1], shares[2], shares[3], shares[4], shares[5...  98.1 us
    reduce_scatter x1, waiting for transfers between devices, body(): lax.psum_scatter(grad_project.astype(jnp.bfloat16), 'frames', scatter_dim...  88.6 us
    reduce_scatter x1, waiting for transfers between devices, body(): lax.psum_scatter(grad_keyval_weight.astype(jnp.bfloat16), 'frames', scatt...  75.7 us
    dot_general x7, matrix products, backward_product(): lax.dot_general(flat, weight, (((1,), (1,)), ((), ())), preferred_element...  44.6 us
    dot_general x7, matrix products, weight_grad(): lax.dot_general(inputs.reshape(-1, inputs.shape[-1]), grad_rows.reshape(-...  41.2 us
    unnamed x149, local copies, waits for them, and re-layouts  35.5 us
  transfers between devices with their start and end apart: 11, of which 8 were waited for; matrix products, arithmetic and copies ran while one was open for 15% of the time, Pallas kernels for 0%

commit v1 on v0

v1 whole, which is shorter than its diff:
```python
from functools import partial

import jax
import jax.numpy as jnp
from jax import lax
from jax.experimental import pallas as pl
from jax.experimental.pallas import tpu as pltpu
from jax.sharding import PartitionSpec as P

HEADS = 8
HEAD_DIM = 128
LEVEL = 1
SCALE = HEAD_DIM ** (-0.5)
LOW = jnp.bfloat16
WIDE = jnp.float32
MIB = 1 << 20


def bit_of(value, place):
    return (value // (1 << place)) % 2


def flipped(value, place):
    return value + (1 << place) - (2 << place) * bit_of(value, place)


def xor_static(constant, value, places):
    total = 0
    for place in range(places):
        bit = bit_of(value, place)
        total = total + ((1 - bit) if (constant >> place) & 1 else bit) * (1 << place)
    return total


def swapped(value, axis, place):
    mask = 1 << place
    return lax.ppermute(value, axis, [(s, s ^ mask) for s in range(lax.axis_size(axis))])


def to_nodes(value):
    half = value.shape[0] // 2
    side = bit_of(lax.axis_index("frames"), LEVEL)
    kept = lax.dynamic_slice_in_dim(value, side * half, half, 0)
    sent = lax.dynamic_slice_in_dim(value, (1 - side) * half, half, 0)
    return kept, swapped(sent, "frames", LEVEL)


def from_nodes(own, back):
    side = bit_of(lax.axis_index("frames"), LEVEL)
    first = jnp.concatenate([own, back], axis=0)
    second = jnp.concatenate([back, own], axis=0)
    return jnp.where(side == 0, first, second)


def layer_norm(values, gain):
    average = jnp.mean(values, axis=-1, keepdims=True)
    centred = values - average
    spread = jnp.mean(centred * centred, axis=-1, keepdims=True)
    return centred * lax.rsqrt(spread + 1e-05) * gain


def norm_back(values, gain, grad_out):
    average = jnp.mean(values, axis=-1, keepdims=True)
    centred = values - average
    spread = jnp.mean(centred * centred, axis=-1, keepdims=True)
    inverse = lax.rsqrt(spread + 1e-05)
    normed = centred * inverse
    scaled = grad_out * gain
    grad = inverse * (
        scaled
        - jnp.mean(scaled, axis=-1, keepdims=True)
        - normed * jnp.mean(scaled * normed, axis=-1, keepdims=True)
    )
    return grad, jnp.sum(grad_out * normed, axis=0)


def matmul(left, right):
    return jnp.dot(left, right, preferred_element_type=WIDE)


def product_back(grad_rows, weight):
    return lax.dot_general(
        grad_rows, weight, (((1,), (1,)), ((), ())), preferred_element_type=WIDE
    )


def weight_grad(inputs, grad_rows):
    return lax.dot_general(
        inputs, grad_rows, (((0,), (0,)), ((), ())), preferred_element_type=WIDE
    )


def dot_nt(left, right):
    return lax.dot_general(left, right, (((1,), (1,)), ((), ())), preferred_element_type=WIDE)


def dot_tn(left, right):
    return lax.dot_general(left, right, (((0,), (0,)), ((), ())), preferred_element_type=WIDE)


def node_rows(ref, head):
    block = ref[:, 0, :, head * HEAD_DIM : (head + 1) * HEAD_DIM]
    return block.reshape(block.shape[0] * block.shape[1], HEAD_DIM)


def valid_keys(count_ref, rows, shape, axis):
    node = pl.program_id(0)
    key = lax.broadcasted_iota(jnp.int32, shape, axis)
    first, second = count_ref[0, node], count_ref[1, node]
    return key < jnp.where(key < rows, first, second + rows)


def attend_kernel(masked, count_ref, q_ref, k_ref, v_ref, out_ref):
    heads = q_ref.shape[3] // HEAD_DIM
    rows = q_ref.shape[2]
    for head in range(heads):
        q, k, v = (node_rows(ref, head) for ref in (q_ref, k_ref, v_ref))
        scores = dot_nt(q, k) * SCALE
        if masked:
            scores = jnp.where(valid_keys(count_ref, rows, scores.shape, 1), scores, -1e30)
        top = jnp.max(scores, axis=1, keepdims=True)
        raised = jnp.exp(scores - top)
        weights = raised / jnp.sum(raised, axis=1, keepdims=True)
        mixed = jnp.dot(weights.astype(LOW), v, preferred_element_type=WIDE)
        out_ref[:, 0, :, head * HEAD_DIM : (head + 1) * HEAD_DIM] = mixed.astype(LOW).reshape(
            2, rows, HEAD_DIM
        )


def attend_back_kernel(masked, count_ref, q_ref, k_ref, v_ref, grad_ref, *outs):
    heads = q_ref.shape[3] // HEAD_DIM
    rows = q_ref.shape[2]
    wide = heads * HEAD_DIM
    places = [(outs[0], 0), (outs[-1], wide if len(outs) == 1 else 0)]
    places.append((outs[-1], places[1][1] + wide))
    for head in range(heads):
        q, k, v, grad = (node_rows(ref, head) for ref in (q_ref, k_ref, v_ref, grad_ref))
        scores = dot_nt(k, q) * SCALE
        if masked:
            scores = jnp.where(valid_keys(count_ref, rows, scores.shape, 0), scores, -1e30)
        top = jnp.max(scores, axis=0, keepdims=True)
        raised = jnp.exp(scores - top)
        weights = raised / jnp.sum(raised, axis=0, keepdims=True)
        grad_weights = dot_nt(v, grad)
        inner = jnp.sum(weights * grad_weights, axis=0, keepdims=True)
        grad_scores = (weights * (grad_weights - inner)).astype(LOW)
        results = (
            dot_tn(grad_scores, k) * SCALE,
            jnp.dot(grad_scores, q, preferred_element_type=WIDE) * SCALE,
            jnp.dot(weights.astype(LOW), grad, preferred_element_type=WIDE),
        )
        for (ref, start), result in zip(places, results):
            start = start + head * HEAD_DIM
            ref[:, 0, :, start : start + HEAD_DIM] = result.astype(LOW).reshape(2, rows, HEAD_DIM)


def column_block(rows, width, column):
    return pl.BlockSpec((2, 1, rows, width), lambda node, *_: (0, node, 0, column))


def attend(counts, queries, keyval, key_column, masked):
    _, nodes, rows, _ = queries.shape
    features = HEADS * HEAD_DIM
    spec = pltpu.PrefetchScalarGridSpec(
        num_scalar_prefetch=1,
        grid=(nodes,),
        in_specs=[column_block(rows, features, c) for c in (0, key_column, key_column + 1)],
        out_specs=column_block(rows, features, 0),
    )
    flops = 4 * nodes * HEADS * (2 * rows) ** 2 * HEAD_DIM
    return pl.pallas_call(
        partial(attend_kernel, masked),
        grid_spec=spec,
        out_shape=jax.ShapeDtypeStruct((2, nodes, rows, features), LOW),
        cost_estimate=pl.CostEstimate(
            flops=flops, bytes_accessed=8 * 2 * nodes * rows * features, transcendentals=flops // 512
        ),
        name="attend",
    )(counts, queries, keyval, keyval)


def attend_back(counts, queries, keyval, key_column, masked, grad_mix):
    _, nodes, rows, _ = queries.shape
    features = HEADS * HEAD_DIM
    widths = (3 * features,) if key_column == 1 else (features, 2 * features)
    spec = pltpu.PrefetchScalarGridSpec(
        num_scalar_prefetch=1,
        grid=(nodes,),
        in_specs=[column_block(rows, features, c) for c in (0, key_column, key_column + 1, 0)],
        out_specs=[column_block(rows, width, 0) for width in widths],
    )
    flops = 10 * nodes * HEADS * (2 * rows) ** 2 * HEAD_DIM
    return pl.pallas_call(
        partial(attend_back_kernel, masked),
        grid_spec=spec,
        out_shape=[jax.ShapeDtypeStruct((2, nodes, rows, width), LOW) for width in widths],
        cost_estimate=pl.CostEstimate(
            flops=flops, bytes_accessed=14 * 2 * nodes * rows * features, transcendentals=flops // 1280
        ),
        name="attend_back",
    )(counts, queries, keyval, keyval, grad_mix)


def feed_kernel(in_ref, grad_ref, up_ref, down_ref, act_ref, grad_hidden_ref, out_ref, grad_in_ref):
    step = pl.program_id(0)

    @pl.when(step == 0)
    def _():
        out_ref[...] = jnp.zeros_like(out_ref)
        grad_in_ref[...] = jnp.zeros_like(grad_in_ref)

    rows = in_ref.shape[0]
    part = rows // 2
    for start in range(0, rows, part):
        here = pl.ds(start, part)
        hidden = jnp.dot(in_ref[here, :], up_ref[...], preferred_element_type=WIDE)
        grad_act = dot_nt(grad_ref[here, :], down_ref[...])
        normal = 0.5 * (1.0 + lax.erf(hidden * 0.7071067811865476))
        density = jnp.exp(-0.5 * hidden * hidden) * 0.3989422804014327
        act = (hidden * normal).astype(LOW)
        grad_hidden = (grad_act * (normal + hidden * density)).astype(LOW)
        act_ref[here, :] = act
        grad_hidden_ref[here, :] = grad_hidden
        out_ref[here, :] += jnp.dot(act, down_ref[...], preferred_element_type=WIDE)
        grad_in_ref[here, :] += dot_nt(grad_hidden, up_ref[...])


def feed(mlp_in, grad_low, mlp_up, mlp_down):
    rows, features = mlp_in.shape
    hidden = mlp_up.shape[1]
    tile = min(512, hidden)
    whole = pl.BlockSpec((rows, features), lambda i: (0, 0))
    return pl.pallas_call(
        feed_kernel,
        grid=(hidden // tile,),
        in_specs=[
            whole,
            whole,
            pl.BlockSpec((features, tile), lambda i: (0, i)),
            pl.BlockSpec((tile, features), lambda i: (i, 0)),
        ],
        out_specs=[
            pl.BlockSpec((rows, tile), lambda i: (0, i)),
            pl.BlockSpec((rows, tile), lambda i: (0, i)),
            whole,
            whole,
        ],
        out_shape=[
            jax.ShapeDtypeStruct((rows, hidden), LOW),
            jax.ShapeDtypeStruct((rows, hidden), LOW),
            jax.ShapeDtypeStruct((rows, features), WIDE),
            jax.ShapeDtypeStruct((rows, features), WIDE),
        ],
        compiler_params=pltpu.CompilerParams(vmem_limit_bytes=40 * MIB),
        cost_estimate=pl.CostEstimate(
            flops=8 * rows * features * hidden,
            bytes_accessed=4 * features * hidden + 12 * rows * hidden,
            transcendentals=2 * rows * hidden,
        ),
        name="feed",
    )(mlp_in, grad_low, mlp_up, mlp_down)


CHUNK = 1024
SHARES = (512, 256, 256)


class Plan:
    def __init__(self, frames, groups, inner):
        self.frames, self.groups = frames, groups
        self.places = frames.bit_length() - 1
        self.group_places = groups.bit_length() - 1
        self.rows = inner // frames
        self.split = groups == 2 and self.rows % 32 == 0
        self.part = self.rows // 2 if self.split else self.rows
        near, far = [("f", 1)], [("f", d) for d in range(2, self.places)]
        if self.split:
            cut, join, add = [("cut", 0)], [("join", 0)], [("add", 0)]
            self.orders = [near + cut + far + join, cut + far + near + join, far + near + add]
        else:
            add = [("add", e) for e in range(self.group_places)]
            self.orders = [near + far + add, far + near + add, far + near + add]
        self.depth = max(len(order) for order in self.orders)
        starts = [0]
        for share in SHARES:
            starts.append(starts[-1] + share)
        self.columns = [(starts[i], SHARES[i]) for i in range(len(SHARES))]
        self.steps = []
        for (start, width), order in zip(self.columns, self.orders):
            fixed, size, steps = {}, self.rows, []
            for kind, place in order:
                free = [d for d in range(1, self.places) if d not in fixed]
                if kind == "f":
                    send, keep = dict(fixed), dict(fixed)
                    send[place], keep[place] = 1, 0
                    send_rows = keep_rows = (0, size)
                    fixed[place] = 0
                    free.remove(place)
                elif kind == "cut":
                    send = keep = dict(fixed)
                    send_rows, keep_rows = (self.part, self.part), (0, self.part)
                    size = self.part
                else:
                    send = keep = dict(fixed)
                    send_rows = keep_rows = (0, size)
                shape = (2,) * len(free) + (send_rows[1], width)
                steps.append((kind, place, send, send_rows, keep, keep_rows, shape))
            self.steps.append(steps)

    def index(self, slot, fixed, rows, columns):
        middle = [fixed.get(d, slice(None)) for d in reversed(range(1, self.places))]
        return tuple([slot] + middle + [pl.ds(*rows), pl.ds(*columns)])


def reduce_kernel(plan, sources, slots, n_in, *refs):
    ins, out_ref, rest = refs[:n_in], refs[n_in], refs[n_in + 1 :]
    raw, grad, turned, sent, held, core_in, load_sem, core_send, core_recv, send_sem, recv_sem = rest[:11]
    lands = rest[11:]
    chunks = len(sources)
    frame, group = lax.axis_index("frames"), lax.axis_index("groups")
    rows, part, places = plan.rows, plan.part, plan.places
    halves = rows // part
    blocks = plan.frames // 2

    ids, count = {}, 0
    for i, steps in enumerate(plan.steps):
        for k in range(len(steps)):
            ids[i, k] = count
            count += 1

    def partner(kind, place):
        if kind == "f":
            return {"frames": flipped(frame, place), "groups": group}
        return {"frames": frame, "groups": flipped(group, place)}

    barrier = pltpu.get_barrier_semaphore()
    everyone = [partner("f", d) for d in range(places)] + [
        partner("g", e) for e in range(plan.group_places)
    ]
    for device in everyone:
        pl.semaphore_signal(barrier, inc=1, device_id=device, device_id_type=pl.DeviceIdType.MESH)
    pl.semaphore_wait(barrier, len(everyone))

    def core_copy(u):
        s = u % 2
        return pltpu.make_async_remote_copy(
            src_ref=sent.at[s],
            dst_ref=core_in.at[s],
            send_sem=core_send.at[s],
            recv_sem=core_recv.at[s],
            device_id=partner("f", 0),
            device_id_type=pl.DeviceIdType.MESH,
        )

    def step_copy(i, k, u):
        kind, place, send, send_rows, _, _, _ = plan.steps[i][k]
        s = u % 2
        return pltpu.make_async_remote_copy(
            src_ref=held.at[plan.index(u % slots, send, send_rows, plan.columns[i])],
            dst_ref=lands[ids[i, k]].at[s],
            send_sem=send_sem.at[ids[i, k], s],
            recv_sem=recv_sem.at[ids[i, k], s],
            device_id=partner(kind, place),
            device_id_type=pl.DeviceIdType.MESH,
        )

    def loads(t, which):
        left, right, column = sources[which]
        s = t % 2
        return (
            pltpu.make_async_copy(ins[left], raw.at[s], load_sem.at[0, s]),
            pltpu.make_async_copy(
                ins[right].at[:, column : column + CHUNK], grad.at[s], load_sem.at[1, s]
            ),
        )

    def row_place(half):
        if halves == 1:
            return 0
        place = bit_of(group, 0)
        return ((1 - place) if half else place) * part

    def finish(i, k, u):
        kind, _, _, _, keep, keep_rows, _ = plan.steps[i][k]
        start, width = plan.columns[i]
        land = lands[ids[i, k]]
        s = u % 2
        if kind == "join":
            mine = held[plan.index(u % slots, keep, (0, part), plan.columns[i])]
            other = land[s]
            for half, value in ((0, mine), (1, other)):
                at = pl.multiple_of(row_place(half), part)
                out_ref[u, pl.ds(at, part), pl.ds(start, width)] = value.astype(WIDE)
        else:
            for half in range(halves):
                source = (halves - 1 - half) * part
                mine = held[plan.index(u % slots, keep, (half * part, part), plan.columns[i])]
                other = land[s, pl.ds(source, part), :]
                at = pl.multiple_of(row_place(half), part)
                out_ref[u, pl.ds(at, part), pl.ds(start, width)] = mine.astype(WIDE) + other.astype(WIDE)

    def advance(i, k, u):
        step_copy(i, k, u).wait()
        if k == len(plan.steps[i]) - 1:
            finish(i, k, u)
            return
        _, _, _, _, keep, keep_rows, _ = plan.steps[i][k]
        at = plan.index(u % slots, keep, keep_rows, plan.columns[i])
        held[at] = held[at] + lands[ids[i, k]][u % 2]
        step_copy(i, k + 1, u).start()

    def turn(s):
        width = 128
        for tile in range(raw.shape[2] // width):
            value = raw[s, :, tile * width : (tile + 1) * width].T
            for piece in range(width // part):
                at = tile * (width // part) + piece
                block, half = at // halves, at % halves
                where = xor_static(block, frame, places)
                row = (where // 2) * rows
                if halves > 1:
                    row = row + xor_static(half, group, 1) * part
                row = pl.multiple_of(row, part)
                turned[where % 2, pl.ds(row, part), :] = value[piece * part : (piece + 1) * part, :]

    def make(t):
        s = t % 2
        for copy in loads(t, 0):
            copy.wait()
        for which in range(1, chunks):

            @pl.when(t + 1 == which)
            def _():
                for copy in loads(t + 1, which):
                    copy.start()

        turn(s)
        piece = 256
        shape = (2,) * (places - 1) + (rows, piece)
        for side in (1, 0):
            for column in range(0, CHUNK, piece):
                value = jnp.dot(
                    turned[side], grad[s, :, column : column + piece], preferred_element_type=WIDE
                ).astype(LOW)
                value = value.reshape(shape)
                at = (slice(None),) * (places - 1) + (slice(None), pl.ds(column, piece))
                if side:
                    sent[(s,) + at] = value
                else:
                    held[(t % slots,) + at] = value
        core_copy(t).start()

    for copy in loads(0, 0):
        copy.start()

    def iteration(t, carry):
        for k in reversed(range(plan.depth)):
            u = t - 2 - k

            @pl.when((u >= 0) & (u < chunks))
            def _():
                for i in range(len(plan.steps)):
                    if k < len(plan.steps[i]):
                        advance(i, k, u)

        u = t - 1

        @pl.when((u >= 0) & (u < chunks))
        def _():
            core_copy(u).wait()
            for i in range(len(plan.steps)):
                at = (slice(None),) * (places - 1) + (slice(None), pl.ds(*plan.columns[i]))
                here = (u % slots,) + at
                held[here] = held[here] + core_in[(u % 2,) + at]
                step_copy(i, 0, u).start()

        @pl.when(t < chunks)
        def _():
            make(t)

        return carry

    lax.fori_loop(0, chunks + plan.depth + 1, iteration, 0)


def reduced(pairs, frames, groups):
    count, inner = pairs[0][0].shape
    plan = Plan(frames, groups, inner)
    operands, sources = [], []
    for left, grad in pairs:
        at = len(operands)
        operands += [left, grad]
        sources += [(at, at + 1, column) for column in range(0, grad.shape[1], CHUNK)]
    chunks, slots = len(sources), plan.depth + 2
    half = (2,) * (plan.places - 1) + (plan.rows, CHUNK)
    steps = [step for steps in plan.steps for step in steps]
    scratch = [
        pltpu.VMEM((2, count, inner), LOW),
        pltpu.VMEM((2, count, CHUNK), LOW),
        pltpu.VMEM((2, inner // 2, count), LOW),
        pltpu.VMEM((2,) + half, LOW),
        pltpu.VMEM((slots,) + half, LOW),
        pltpu.VMEM((2,) + half, LOW),
        pltpu.SemaphoreType.DMA((2, 2)),
        pltpu.SemaphoreType.DMA((2,)),
        pltpu.SemaphoreType.DMA((2,)),
        pltpu.SemaphoreType.DMA((len(steps), 2)),
        pltpu.SemaphoreType.DMA((len(steps), 2)),
    ] + [pltpu.VMEM((2,) + step[-1], LOW) for step in steps]
    result = pl.pallas_call(
        partial(reduce_kernel, plan, sources, slots, len(operands)),
        out_shape=jax.ShapeDtypeStruct((chunks, plan.rows, CHUNK), WIDE),
        in_specs=[pl.BlockSpec(memory_space=pl.ANY)] * len(operands),
        out_specs=pl.BlockSpec(memory_space=pltpu.VMEM),
        scratch_shapes=scratch,
        compiler_params=pltpu.CompilerParams(
            collective_id=0, has_side_effects=True, vmem_limit_bytes=48 * MIB
        ),
        cost_estimate=pl.CostEstimate(
            flops=2 * count * inner * CHUNK * chunks * 5,
            bytes_accessed=4 * count * CHUNK * chunks,
            transcendentals=0,
        ),
        name="reduce",
    )(*operands)
    outs, at = [], 0
    for _, grad in pairs:
        parts = grad.shape[1] // CHUNK
        outs.append(jnp.concatenate([result[at + i] for i in range(parts)], axis=1))
        at += parts
    return outs


def body(
    parents,
    children,
    child_counts,
    out_grad,
    child_gain,
    cross_gain,
    cross_query,
    cross_keyval,
    cross_output,
    self_gain,
    self_project,
    self_output,
    mlp_gain,
    mlp_up,
    mlp_down,
):
    clips, half_rows, features = parents.shape
    nodes = clips // 2
    frames, groups = lax.axis_size("frames"), lax.axis_size("groups")
    frame = lax.axis_index("frames")
    other = flipped(frame, LEVEL)
    side = bit_of(frame, LEVEL)
    child_own, child_got = to_nodes(children)
    parent_own, parent_got = to_nodes(parents)
    grad_own, grad_got = to_nodes(out_grad)
    mine = lax.dynamic_slice_in_dim(child_counts, side * nodes, nodes, 0)
    counts = jnp.stack(
        [
            lax.dynamic_slice_in_dim(mine, frame, 1, 1)[:, 0],
            lax.dynamic_slice_in_dim(mine, other, 1, 1)[:, 0],
        ]
    )

    def flat(value):
        return value.reshape(-1, value.shape[-1])

    def rows4(value):
        return value.reshape(2, nodes, half_rows, value.shape[-1])

    def join(own, got):
        return flat(jnp.concatenate([own, got], axis=0))

    gain_child = child_gain.astype(WIDE)
    gain_cross = cross_gain.astype(WIDE)
    gain_self = self_gain.astype(WIDE)
    gain_mlp = mlp_gain.astype(WIDE)

    child_latents = join(child_own, child_got).astype(WIDE)
    latents = join(parent_own, parent_got).astype(WIDE)
    grad_low = join(grad_own, grad_got)

    child_in = layer_norm(child_latents, gain_child).astype(LOW)
    keyval = matmul(child_in, cross_keyval).astype(LOW)
    cross_in = layer_norm(latents, gain_cross).astype(LOW)
    queries = matmul(cross_in, cross_query).astype(LOW)
    cross_mixed = flat(attend(counts, rows4(queries), rows4(keyval), 0, True))
    after_cross = latents + matmul(cross_mixed, cross_output)
    self_in = layer_norm(after_cross, gain_self).astype(LOW)
    projected = matmul(self_in, self_project).astype(LOW)
    self_mixed = flat(attend(counts, rows4(projected), rows4(projected), 1, False))
    after_self = after_cross + matmul(self_mixed, self_output)
    mlp_in = layer_norm(after_self, gain_mlp).astype(LOW)
    activated, grad_hidden, fed, grad_mlp_in = feed(mlp_in, grad_low, mlp_up, mlp_down)
    top = (after_self + fed).astype(LOW).reshape(2, nodes, half_rows, features)
    top_latents = from_nodes(top[0], swapped(top[1], "frames", LEVEL))

    grad_down = weight_grad(activated, grad_low).astype(LOW)
    share_down = lax.psum_scatter(grad_down, "frames", scatter_dimension=0, tiled=True)

    grad_norm, gain_grad_mlp = norm_back(after_self, gain_mlp, grad_mlp_in)
    grad_after_self = grad_low.astype(WIDE) + grad_norm
    grad_self_out = grad_after_self.astype(LOW)
    grad_self_mix = product_back(grad_self_out, self_output).astype(LOW)
    (grad_projected,) = attend_back(
        counts, rows4(projected), rows4(projected), 1, False, rows4(grad_self_mix)
    )
    grad_projected = flat(grad_projected)
    grad_norm, gain_grad_self = norm_back(
        after_cross, gain_self, product_back(grad_projected, self_project)
    )
    grad_after_cross = grad_after_self + grad_norm
    grad_cross_out = grad_after_cross.astype(LOW)
    grad_cross_mix = product_back(grad_cross_out, cross_output).astype(LOW)
    grad_queries, grad_keyval = attend_back(
        counts, rows4(queries), rows4(keyval), 0, True, rows4(grad_cross_mix)
    )
    grad_queries, grad_keyval = flat(grad_queries), flat(grad_keyval)
    grad_norm, gain_grad_cross = norm_back(
        latents, gain_cross, product_back(grad_queries, cross_query)
    )
    grad_parents = rows4(grad_after_cross + grad_norm)
    grad_norm, gain_grad_child = norm_back(
        child_latents, gain_child, product_back(grad_keyval, cross_keyval)
    )
    grad_children = rows4(grad_norm)
    parents_back = swapped(grad_parents[1].astype(LOW), "frames", LEVEL).astype(WIDE)
    children_back = swapped(grad_children[1].astype(LOW), "frames", LEVEL).astype(WIDE)

    total_up, total_self_out, total_project, total_cross_out, total_query, total_keyval = reduced(
        [
            (mlp_in, grad_hidden),
            (self_mixed, grad_self_out),
            (self_in, grad_projected),
            (cross_mixed, grad_cross_out),
            (cross_in, grad_queries),
            (child_in, grad_keyval),
        ],
        frames,
        groups,
    )
    total_down = share_down
    for place in range(groups.bit_length() - 1):
        total_down = total_down + swapped(total_down, "groups", place)
    total_down = total_down.astype(WIDE)
    gains = jnp.stack([gain_grad_child, gain_grad_cross, gain_grad_self, gain_grad_mlp])
    gains = lax.psum(gains, ("frames", "groups"))
    width = features // frames
    gains = lax.dynamic_slice_in_dim(gains, frame * width, width, 1)
    return (
        top_latents,
        from_nodes(grad_parents[0], parents_back),
        from_nodes(grad_children[0], children_back),
        gains[0],
        gains[1],
        total_query,
        total_keyval,
        total_cross_out,
        gains[2],
        total_project,
        total_self_out,
        gains[3],
        total_up,
        total_down,
    )


def solution(mesh):
    rows = P("groups", "frames", None)
    shard, shard2 = P("frames"), P("frames", None)
    return jax.shard_map(
        body,
        mesh=mesh,
        in_specs=(rows, rows, P("groups", None), rows) + (P(),) * 11,
        out_specs=(
            rows,
            rows,
            rows,
            shard,
            shard,
            shard2,
            shard2,
            shard2,
            shard,
            shard2,
            shard2,
            shard,
            shard2,
            shard2,
        ),
        check_vma=False,
    )
```

time: 977 us -> 392 us (0.40)
  waiting for transfers between devices: 532 us -> 17 us
  Pallas kernels: 0 us -> 180 us
  matrix products: 151 us -> 48.9 us
  blocking collectives: 129 us -> 62.4 us
  local copies, waits for them, and re-layouts: 68.4 us -> 19 us
  other arithmetic: 69.3 us -> 33.5 us
    reduce_scatter x7 -> x1, waiting for transfers between devices: 273 us -> 0.01 us  [body(): lax.psum_scatter(grad_down, 'frames', scatter_dimension=0, tiled=True)]
    ppermute x4 -> x7, waiting for transfers between devices: 259 us -> 17 us  [swapped(): lax.ppermute(value, axis, [(s, s ^ mask) for s in range(lax.axis_size(axi...]
    pallas_call x0 -> x6, Pallas kernels: none -> 180 us  [the longest x1 124 us: reduced(): pl.pallas_call(partial(reduce_kernel, plan, sources, slots, len(operands)...]
    dot_general x33 -> x11, matrix products: 151 us -> 48.9 us  [the longest x5 21.7 us: product_back(): lax.dot_general(grad_rows, weight, (((1,), (1,)), ((), ())), preferred_el...]
    psum x1, blocking collectives: 98.1 us -> 62.4 us  [body(): gains = lax.psum(gains, ('frames', 'groups'))]
    unnamed x1 -> x0, blocking collectives: 30.5 us -> none
    unnamed x149 -> x82, local copies, waits for them, and re-layouts: 35.5 us -> 6.77 us
    convert_element_type x13, other arithmetic: 30 us -> 11.5 us  [the longest x1 2.5 us: body(): grad_self_out = grad_after_self.astype(LOW)]
  transfers between devices with their start and end apart: 11 -> 8, of which waited for: 8 -> 3; matrix products, arithmetic and copies ran while one was open for 15% -> 21% of each run, Pallas kernels for 0% -> 38%
where the time goes in v1:
time: 392 us; the launch traced here: 387 us
  Pallas kernels  180 us (46%)
  blocking collectives  62.4 us (16%)
  matrix products  48.9 us (12%)
  other arithmetic  33.5 us (9%)
  local copies, waits for them, and re-layouts  19 us (5%)
  waiting for transfers between devices  17 us (4%)
  between operations  14.9 us (4%)
  starting transfers between devices  10.8 us (3%)
    pallas_call x1, Pallas kernels, reduced(): pl.pallas_call(partial(reduce_kernel, plan, sources, slots, len(operands)...  124 us
    psum x1, blocking collectives, body(): gains = lax.psum(gains, ('frames', 'groups'))  62.4 us
    pallas_call x1, Pallas kernels, feed(): pl.pallas_call(feed_kernel, grid=(hidden // tile,), in_specs=[whole, whol...  23.1 us
    dot_general x5, matrix products, product_back(): lax.dot_general(grad_rows, weight, (((1,), (1,)), ((), ())), preferred_el...  21.7 us
    pallas_call x2, Pallas kernels, attend_back(): pl.pallas_call(partial(attend_back_kernel, masked), grid_spec=spec, out_s...  20.9 us
    dot_general x5, matrix products, matmul(): return jnp.dot(left, right, preferred_element_type=WIDE)  18 us
    ppermute x7, waiting for transfers between devices, swapped(): lax.ppermute(value, axis, [(s, s ^ mask) for s in range(lax.axis_size(axi...  17 us
    pallas_call x2, Pallas kernels, attend(): pl.pallas_call(partial(attend_kernel, masked), grid_spec=spec, out_shape=...  12.6 us
  transfers between devices with their start and end apart: 8, of which 3 were waited for; matrix products, arithmetic and copies ran while one was open for 21% of the time, Pallas kernels for 38%

profile of v1, /device:TPU:0, one launch (start us, length us, event | category | flops | bytes accessed | tf_op | source)
XLA Modules:
  0.0 386.7 jit_solution(10532224450687958144)
XLA Ops:
  7.3 2.2 constant_dynamic-slice_fusion.6
  9.6 3.0 collective-permute-start
  12.6 0.9 constant_dynamic-slice_fusion.4
  13.6 1.2 constant_dynamic-slice_fusion.2
  14.7 1.9 collective-permute-start.2
  16.9 0.6 pad_add_fusion.count_ref
  17.5 8.2 %collective-permute-done = bf16[2,128,1024]{2,1,0:T(8,128)(2,1)} collective-permute-done((bf16[2,128,1024]{2,1,0:T(8,128)(2,1)}, bf16[2,128,1024]{2,1,0:T(8,128)(2,1)}, u32[]{:S(2)}, u32[]{:S(2)}) %collective-permute-start) | collective-permute-done | bytes 524320 | tf_op jit(solution)/shard_map/ppermute | solution.py:37
  25.7 1.3 convert_reduce_fusion
  27.0 1.5 fusion.2
  28.4 8.5 %collective-permute-done.1 = bf16[2,128,1024]{2,1,0:T(8,128)(2,1)} collective-permute-done((bf16[2,128,1024]{2,1,0:T(8,128)(2,1)}, bf16[2,128,1024]{2,1,0:T(8,128)(2,1)}, u32[]{:S(2)}, u32[]{:S(2)}) %collective-permute-start.1) | collective-permute-done | bytes 524320 | tf_op jit(solution)/shard_map/ppermute | solution.py:37
  37.0 1.3 convert_reduce_fusion.1
  38.2 1.5 multiply_reduce_fusion.8
  39.7 1.4 fusion.8.refs_8_
  41.1 2.2 convolution_convert_fusion.5
  43.4 1.4 multiply_convert_fusion.2.refs_10_
  44.8 3.7 convolution_convert_fusion.2
  48.5 6.6 %attend.2 = bf16[2,2,128,1024]{3,2,1,0:T(8,128)(2,1)} custom-call(s32[2,2]{1,0:T(2,128)} %pad_add_fusion.count_ref, bf16[2,2,128,1024]{3,2,1,0:T(8,128)(2,1)} %bitcast.142, bf16[2,2,128,2048]{3,2,1,0:T(8,128)(2,1)} %bitcast.136, bf16[2,2,128,2048]{3,2,1,0:T(8,128)(2,1)} %bitcast.137), custom_call_target="tpu_custom_call" | custom-call | flops 536870912 | bytes 4194304 | tf_op jit(solution)/shard_map/attend/pallas_call | solution.py:171
  55.1 1.3 pad_maximum_fusion
  56.5 3.3 fusion.19
  59.8 0.3 multiply_reduce_fusion.7
  60.1 0.9 copy-done.12
  61.4 4.9 %convolution_convert_fusion.1 = bf16[512,3072]{1,0:T(8,128)(2,1)} fusion(bf16[512,1024]{1,0:T(8,128)(2,1)S(1)} %multiply_convert_fusion.1.refs_4_, bf16[1024,3072]{1,0:T(8,128)(2,1)S(1)} %bitcast.156), kind=kOutput, calls=%fused_computation.1 | convolution fusion | flops 3222798336 | bytes 10485760 | tf_op jit(solution)/shard_map/dot_general | solution.py:78
  66.3 6.0 %attend.3 = bf16[2,2,128,1024]{3,2,1,0:T(8,128)(2,1)} custom-call(s32[2,2]{1,0:T(2,128)} %pad_add_fusion.count_ref, bf16[2,2,128,3072]{3,2,1,0:T(8,128)(2,1)} %bitcast.130, bf16[2,2,128,3072]{3,2,1,0:T(8,128)(2,1)} %bitcast.131, bf16[2,2,128,3072]{3,2,1,0:T(8,128)(2,1)} %bitcast.132), custom_call_target="tpu_custom_call" | custom-call | flops 536870912 | bytes 4194304 | tf_op jit(solution)/shard_map/attend/pallas_call | solution.py:171
  72.3 3.9 %fusion.20 = (f32[512]{0:T(512)S(1)}, f32[512,1024]{1,0:T(8,128)S(1)}) fusion(f32[512,1024]{1,0:T(8,128)} %copy-done.12, bf16[512,1024]{1,0:T(8,128)(2,1)} %bitcast.128, bf16[1024,1024]{1,0:T(8,128)(2,1)} %param.26), kind=kOutput, calls=%fused_computation.110 | convolution fusion | flops 1074789888 | bytes 7342080 | tf_op jit(solution)/shard_map/dot_general | solution.py:78
  76.2 0.3 multiply_reduce_fusion.6
  76.9 0.7 copy-done.23
  77.6 1.1 pad_maximum_fusion.2
  78.8 23.1 %feed.1 = (bf16[512,4096]{1,0:T(8,128)(2,1)S(1)}, bf16[512,4096]{1,0:T(8,128)(2,1)}, f32[512,1024]{1,0:T(8,128)S(1)}, f32[512,1024]{1,0:T(8,128)S(1)}) custom-call(bf16[512,1024]{1,0:T(8,128)(2,1)S(1)} %multiply_convert_fusion.in_ref.refs_0_, bf16[512,1024]{1,0:T(8,128)(2,1)S(1)} %bitcast.124, bf16[1024,4096]{1,0:T(8,128)(2,1)} %up_ref.1, ...), custom_call_target="tpu_custom_call" | custom-call | flops 17179869184 | bytes 41943040 | tf_op jit(solution)/shard_map/feed/pallas_call | solution.py:233
  101.8 0.8 multiply_reduce_fusion
  102.7 1.1 copy-done.11
  103.8 2.5 fusion.17
  106.3 2.3 convolution_convert_fusion.4
  108.6 10.2 %attend_back.2 = bf16[2,2,128,3072]{3,2,1,0:T(8,128)(2,1)} custom-call(s32[2,2]{1,0:T(2,128)} %pad_add_fusion.count_ref, bf16[2,2,128,3072]{3,2,1,0:T(8,128)(2,1)} %bitcast.133, bf16[2,2,128,3072]{3,2,1,0:T(8,128)(2,1)} %bitcast.134, bf16[2,2,128,3072]{3,2,1,0:T(8,128)(2,1)} %bitcast.135, bf16[2,2,128,1024]{3,2,1,0:T(8,128)(2,1)} %bitcast.148), custom_call_target="tpu_custom_call" | custom-call | flops 1342177280 | bytes 7340032 | tf_op jit(solution)/shard_map/attend_back/pallas_call | solution.py:193
  118.8 2.3 fusion.18
  121.0 2.0 collective-permute-start.3
  123.1 9.2 %convolution_convert_fusion = bf16[4096,1024]{1,0:T(8,128)(2,1)} fusion(bf16[512,4096]{1,0:T(8,128)(2,1)} %copy-done.11, bf16[512,1024]{1,0:T(8,128)(2,1)S(1)} %bitcast.125), kind=kOutput, calls=%fused_computation | convolution fusion | flops 4299161600 | bytes 13631488 | tf_op jit(solution)/shard_map/dot_general | solution.py:88
  132.4 8.3 %multiply_reduce_fusion.1 = (f32[1024]{0:T(1024)S(1)}, f32[512]{0:T(512)S(1)}, f32[512]{0:T(512)S(1)}, f32[512,1024]{1,0:T(8,128)S(1)}) fusion(f32[512,1024]{1,0:T(8,128)} %copy-done.12, f32[512]{0:T(512)S(1)} %add_rsqrt_fusion.1, f32[512]{0:T(512)S(1)} %broadcast_multiply_fusion.9, f32[1024]{0:T(1024)S(1)} %convert_element_type.103, ...), kind=kOutput, calls=%fused_computation.25 | convolution fusion | flops 3225417728 | bytes 13647872 | tf_op jit(solution)/shard_map/dot_general | solution.py:82
  140.7 2.0 fusion.16
  142.8 2.3 convolution_convert_fusion.3
  145.1 10.7 %attend_back.3 = (bf16[2,2,128,1024]{3,2,1,0:T(8,128)(2,1)}, bf16[2,2,128,2048]{3,2,1,0:T(8,128)(2,1)}) custom-call(s32[2,2]{1,0:T(2,128)} %pad_add_fusion.count_ref, bf16[2,2,128,1024]{3,2,1,0:T(8,128)(2,1)} %bitcast.143, bf16[2,2,128,2048]{3,2,1,0:T(8,128)(2,1)} %bitcast.138, bf16[2,2,128,2048]{3,2,1,0:T(8,128)(2,1)} %bitcast.139, ...), custom_call_target="tpu_custom_call" | custom-call | flops 1342177280 | bytes 7340032 | tf_op jit(solution)/shard_map/attend_back/pallas_call | solution.py:193
  155.8 5.7 %multiply_reduce_fusion.2 = (f32[1024]{0:T(1024)S(1)}, f32[512]{0:T(512)S(1)}, f32[512]{0:T(512)S(1)}, f32[512,1024]{1,0:T(8,128)S(1)}) fusion(f32[512]{0:T(512)S(1)} %rsqrt_bitcast_fusion, f32[512]{0:T(512)S(1)} %get-tuple-element.69, bf16[2,128,1024]{2,1,0:T(8,128)(2,1)} %collective-permute-done.1, bf16[2,128,1024]{2,1,0:T(8,128)(2,1)S(1)} %copy-done.17, ...), kind=kOutput, calls=%fused_computation.26 | convolution fusion | flops 2152724480 | bytes 9453568 | tf_op jit(solution)/shard_map/dot_general | solution.py:82
  161.5 1.8 subtract_multiply_fusion
  163.4 1.0 slice.120
  164.5 3.1 fusion.13
  167.7 1.9 fusion.12
  169.6 1.3 copy-done.21
  170.9 0.9 slice.121
  171.8 1.6 collective-permute-start.4
  173.4 62.4 %psum.7 = f32[4,1024]{1,0:T(4,128)S(1)} all-reduce(f32[4,1024]{1,0:T(4,128)S(1)} %pad_maximum_fusion.6), channel_id=1, replica_groups=mesh['frames'=16,'groups'=2] {'frames','groups'}, use_global_device_ids=true, to_apply=%region_20.21 | all-reduce | flops 4096 | bytes 32768 | tf_op jit(solution)/shard_map/psum | solution.py:650
  235.9 1.2 copy-done.9
  237.1 1.2 copy-done.10
  238.3 123.7 %reduce.9 = f32[12,64,1024]{2,1,0:T(8,128)} custom-call(bf16[512,1024]{1,0:T(8,128)(2,1)S(1)} %copy-done.5, bf16[512,4096]{1,0:T(8,128)(2,1)} %get-tuple-element.24.refs_1_, bf16[512,1024]{1,0:T(8,128)(2,1)S(1)} %bitcast.129, bf16[512,1024]{1,0:T(8,128)(2,1)S(1)} %copy-done.7, bf16[512,1024]{1,0:T(8,128)(2,1)S(1)} %copy-done.3, bf16[512,3072]{1,0:T(8,128)(2,1)} %bitcast.145, ...), custom_call_target="tpu_custom_call" | custom-call | flops 64424509440 | bytes 25165824 | tf_op jit(solution)/shard_map/reduce/pallas_call | solution.py:510
  362.1 3.0 slice_bitcast_fusion.3
  365.0 0.8 pad_maximum_fusion.5
  365.9 1.0 pad_maximum_fusion.3
  366.9 0.9 pad_maximum_fusion.4
  367.8 1.9 collective-permute-start.6
  369.8 0.5 slice_bitcast_fusion.12
  370.3 1.2 convert_element_type.117
  371.5 1.2 convert_element_type.115
  372.8 2.3 maximum_select_fusion.2
  375.2 1.6 maximum_select_fusion.1
  376.8 1.5 maximum_select_fusion
  378.5 1.0 add_convert_fusion.1
  (115 shorter events, 1.9 us)
Async XLA Ops:
  7.2 33.9 %copy-start = (bf16[1024,1024]{1,0:T(8,128)(2,1)S(1)}, bf16[1024,1024]{1,0:T(8,128)(2,1)}, u32[]{:S(2)}) copy-start(bf16[1024,1024]{1,0:T(8,128)(2,1)} %param.21) | copy-start | bytes 6291460
  7.2 360.6 %reduce-scatter.2.cloned.1.call-start = ((), (), s32[]{:S(2)}) async-start(), calls=%async_computation.1 | async-start | bytes 8912896 | tf_op jit(solution)/shard_map/reduce_scatter | solution.py:602
  7.3 5.3 %copy-start.27 = (bf16[4,128,1024]{2,1,0:T(8,128)(2,1)S(1)}, bf16[4,128,1024]{2,1,0:T(8,128)(2,1)}, u32[]{:S(2)}) copy-start(bf16[4,128,1024]{2,1,0:T(8,128)(2,1)} %param.16) | copy-start | bytes 3145732
  7.3 6.3 %copy-start.28 = (bf16[4,128,1024]{2,1,0:T(8,128)(2,1)S(1)}, bf16[4,128,1024]{2,1,0:T(8,128)(2,1)}, u32[]{:S(2)}) copy-start(bf16[4,128,1024]{2,1,0:T(8,128)(2,1)} %param.18) | copy-start | bytes 3145732
  9.6 45.5 %copy-start.14 = (bf16[2,128,1024]{2,1,0:T(8,128)(2,1)}, bf16[2,128,1024]{2,1,0:T(8,128)(2,1)S(1)}, u32[]{:S(2)}) copy-start(bf16[2,128,1024]{2,1,0:T(8,128)(2,1)S(1)} %get-tuple-element.63) | copy-start | bytes 1572868
  9.6 7.1 %copy-start.30 = (bf16[1024]{0:T(1024)(128)(2,1)S(1)}, bf16[1024]{0:T(1024)(128)(2,1)}, u32[]{:S(2)}) copy-start(bf16[1024]{0:T(1024)(128)(2,1)} %param.19) | copy-start | bytes 6148
  9.6 7.1 %copy-start.31 = (bf16[1024]{0:T(1024)(128)(2,1)S(1)}, bf16[1024]{0:T(1024)(128)(2,1)}, u32[]{:S(2)}) copy-start(bf16[1024]{0:T(1024)(128)(2,1)} %param.20) | copy-start | bytes 6148
  9.6 7.1 %copy-start.32 = (bf16[1024]{0:T(1024)(128)(2,1)S(1)}, bf16[1024]{0:T(1024)(128)(2,1)}, u32[]{:S(2)}) copy-start(bf16[1024]{0:T(1024)(128)(2,1)} %param.24) | copy-start | bytes 6148
  9.6 7.1 %copy-start.33 = (bf16[1024]{0:T(1024)(128)(2,1)S(1)}, bf16[1024]{0:T(1024)(128)(2,1)}, u32[]{:S(2)}) copy-start(bf16[1024]{0:T(1024)(128)(2,1)} %param.27) | copy-start | bytes 6148
  9.6 7.1 %copy-start.34 = (s32[4,16]{1,0:T(4,128)S(1)}, s32[4,16]{1,0:T(4,128)}, u32[]{:S(2)}) copy-start(s32[4,16]{1,0:T(4,128)} %param.17) | copy-start | bytes 772
  9.6 16.1 %collective-permute-start = (bf16[2,128,1024]{2,1,0:T(8,128)(2,1)}, bf16[2,128,1024]{2,1,0:T(8,128)(2,1)}, u32[]{:S(2)}, u32[]{:S(2)}) collective-permute-start(bf16[2,128,1024]{2,1,0:T(8,128)(2,1)} %get-tuple-element.64), channel_id=1, source_target_pairs={{0,4},{2,6},{4,0},{6,2},{8,12},{10,14},{12,8},{14,10},{16,20},{18,... | collective-permute-start | bytes 1572872 | tf_op jit(solution)/shard_map/ppermute | solution.py:37
  13.5 29.9 %copy-start.16 = (bf16[2,128,1024]{2,1,0:T(8,128)(2,1)}, bf16[2,128,1024]{2,1,0:T(8,128)(2,1)S(1)}, u32[]{:S(2)}) copy-start(bf16[2,128,1024]{2,1,0:T(8,128)(2,1)S(1)} %get-tuple-element.61) | copy-start | bytes 1572868
  13.5 23.4 %collective-permute-start.1 = (bf16[2,128,1024]{2,1,0:T(8,128)(2,1)}, bf16[2,128,1024]{2,1,0:T(8,128)(2,1)}, u32[]{:S(2)}, u32[]{:S(2)}) collective-permute-start(bf16[2,128,1024]{2,1,0:T(8,128)(2,1)} %get-tuple-element.62), channel_id=1, source_target_pairs={{0,4},{2,6},{4,0},{6,2},{8,12},{10,14},{12,8},{14,10},{16,20},{18,... | collective-permute-start | bytes 1572872 | tf_op jit(solution)/shard_map/ppermute | solution.py:37
  14.7 62.2 %collective-permute-start.2 = (bf16[2,128,1024]{2,1,0:T(8,128)(2,1)}, bf16[2,128,1024]{2,1,0:T(8,128)(2,1)}, u32[]{:S(2)}, u32[]{:S(2)}) collective-permute-start(bf16[2,128,1024]{2,1,0:T(8,128)(2,1)} %get-tuple-element.60), channel_id=1, source_target_pairs={{0,4},{2,6},{4,0},{6,2},{8,12},{10,14},{12,8},{14,10},{16,20},{18,... | collective-permute-start | bytes 1572872 | tf_op jit(solution)/shard_map/ppermute | solution.py:37
  41.1 2.3 copy-start.25
  41.1 3.7 copy-start.35
  44.8 3.7 copy-start.26
  55.1 1.4 copy-start.8
  55.1 6.3 %slice-start.2 = ((s8[6291456]{0:T(1024)(128)(4,1)}), s8[4194304]{0:T(1024)(128)(4,1)S(1)}, s32[]{:S(2)}) async-start(s8[6291456]{0:T(1024)(128)(4,1)} %bitcast.155), calls=%async_computation.4 | async-start | bytes 8388608
  56.5 5.0 %slice-start.3 = ((s8[6291456]{0:T(1024)(128)(4,1)}), s8[2097152]{0:T(1024)(128)(4,1)S(1)}, s32[]{:S(2)}) async-start(s8[6291456]{0:T(1024)(128)(4,1)} %bitcast.155), calls=%async_computation.5 | async-start | bytes 4194304
  59.7 1.3 copy-start.12
  61.4 4.9 %copy-start.2 = (bf16[512,1024]{1,0:T(8,128)(2,1)}, bf16[512,1024]{1,0:T(8,128)(2,1)S(1)}, u32[]{:S(2)}) copy-start(bf16[512,1024]{1,0:T(8,128)(2,1)S(1)} %multiply_convert_fusion.1.refs_4_) | copy-start | bytes 3145732
  76.6 1.0 copy-start.23
  76.9 24.9 %copy-start.4 = (bf16[512,1024]{1,0:T(8,128)(2,1)}, bf16[512,1024]{1,0:T(8,128)(2,1)S(1)}, u32[]{:S(2)}) copy-start(bf16[512,1024]{1,0:T(8,128)(2,1)S(1)} %multiply_convert_fusion.in_ref.refs_0_) | copy-start | bytes 3145732
  101.8 1.9 copy-start.11
  103.8 2.5 copy-start.36
  106.3 2.3 copy-start.6
  121.0 251.7 %collective-permute-start.3 = (bf16[2,128,1024]{2,1,0:T(8,128)(2,1)}, bf16[2,128,1024]{2,1,0:T(8,128)(2,1)}, u32[]{:S(2)}, u32[]{:S(2)}) collective-permute-start(bf16[2,128,1024]{2,1,0:T(8,128)(2,1)} %bitcast.13), channel_id=1, source_target_pairs={{0,4},{2,6},{4,0},{6,2},{8,12},{10,14},{12,8},{14,10},{16,20},{18,... | collective-permute-start | bytes 1572872 | tf_op jit(solution)/shard_map/ppermute | solution.py:37
  132.3 8.4 %copy-start.13 = (f32[512,1024]{1,0:T(8,128)S(1)}, f32[512,1024]{1,0:T(8,128)}, u32[]{:S(2)}) copy-start(f32[512,1024]{1,0:T(8,128)} %copy-done.12) | copy-start | bytes 6291460
  132.3 8.4 %copy-start.19 = (f32[512,1024]{1,0:T(8,128)S(1)}, f32[512,1024]{1,0:T(8,128)}, u32[]{:S(2)}) copy-start(f32[512,1024]{1,0:T(8,128)} %get-tuple-element.43) | copy-start | bytes 6291460
  140.7 2.1 copy-start.37
  142.8 2.3 copy-start.24
  145.1 10.7 %copy-start.17 = (bf16[2,128,1024]{2,1,0:T(8,128)(2,1)S(1)}, bf16[2,128,1024]{2,1,0:T(8,128)(2,1)}, u32[]{:S(2)}) copy-start(bf16[2,128,1024]{2,1,0:T(8,128)(2,1)} %copy-done.16) | copy-start | bytes 1572868
  161.5 3.0 copy-start.15
  161.5 3.0 copy-start.38
  163.3 4.3 %copy-start.20 = (f32[512,1024]{1,0:T(8,128)}, f32[512,1024]{1,0:T(8,128)S(1)}, u32[]{:S(2)}) copy-start(f32[512,1024]{1,0:T(8,128)S(1)} %subtract_multiply_fusion) | copy-start | bytes 6291460
  164.3 206.0 %collective-permute-start.5 = (bf16[2,128,1024]{2,1,0:T(8,128)(2,1)}, bf16[2,128,1024]{2,1,0:T(8,128)(2,1)}, u32[]{:S(2)}, u32[]{:S(2)}) collective-permute-start(bf16[2,128,1024]{2,1,0:T(8,128)(2,1)} %bitcast.22), channel_id=1, source_target_pairs={{0,4},{2,6},{4,0},{6,2},{8,12},{10,14},{12,8},{14,10},{16,20},{18,... | collective-permute-start | bytes 1572872 | tf_op jit(solution)/shard_map/ppermute | solution.py:37
  164.5 3.1 copy-start.18
  167.7 68.2 %copy-start.3 = (bf16[512,1024]{1,0:T(8,128)(2,1)S(1)}, bf16[512,1024]{1,0:T(8,128)(2,1)}, u32[]{:S(2)}) copy-start(bf16[512,1024]{1,0:T(8,128)(2,1)} %copy-done.2) | copy-start | bytes 3145732
  167.7 68.2 %copy-start.5 = (bf16[512,1024]{1,0:T(8,128)(2,1)S(1)}, bf16[512,1024]{1,0:T(8,128)(2,1)}, u32[]{:S(2)}) copy-start(bf16[512,1024]{1,0:T(8,128)(2,1)} %copy-done.4) | copy-start | bytes 3145732
  167.7 68.2 %copy-start.7 = (bf16[512,1024]{1,0:T(8,128)(2,1)S(1)}, bf16[512,1024]{1,0:T(8,128)(2,1)}, u32[]{:S(2)}) copy-start(bf16[512,1024]{1,0:T(8,128)(2,1)} %copy-done.6) | copy-start | bytes 3145732
  169.6 1.3 copy-start.21
  171.8 199.7 %collective-permute-start.4 = (bf16[2,128,1024]{2,1,0:T(8,128)(2,1)}, bf16[2,128,1024]{2,1,0:T(8,128)(2,1)}, u32[]{:S(2)}, u32[]{:S(2)}) collective-permute-start(bf16[2,128,1024]{2,1,0:T(8,128)(2,1)} %bitcast.19), channel_id=1, source_target_pairs={{0,4},{2,6},{4,0},{6,2},{8,12},{10,14},{12,8},{14,10},{16,20},{18,... | collective-permute-start | bytes 1572872 | tf_op jit(solution)/shard_map/ppermute | solution.py:37
  235.9 1.2 copy-start.9
  237.1 1.2 copy-start.10
  367.8 10.7 %collective-permute-start.6 = (bf16[256,1024]{1,0:T(8,128)(2,1)}, bf16[256,1024]{1,0:T(8,128)(2,1)S(1)}, u32[]{:S(2)}, u32[]{:S(2)}) collective-permute-start(bf16[256,1024]{1,0:T(8,128)(2,1)} %reduce-scatter.2.cloned.1.call-done), channel_id=1, source_target_pairs={{0,1},{1,0},{2,3},{3,2},{4,5},{5,4},{6,7},{7,6},{8,9},{9,8},{10,11... | collective-permute-start | bytes 1572872 | tf_op jit(solution)/shard_map/ppermute | solution.py:37
  370.3 2.5 copy-start.22
  371.5 3.6 slice-start
  375.1 1.6 slice-start.1
  376.8 1.8 copy-start.29
  376.8 2.8 copy-start.1
Sparse Core Ops, SparseCore 0:
  132.5 109.7 reduce-scatter.1

commit v2 on v1

--- a/solution.py
+++ b/solution.py
@@ -313,9 +313,11 @@
 
 
 def reduce_kernel(plan, sources, slots, n_in, *refs):
-    ins, out_ref, rest = refs[:n_in], refs[n_in], refs[n_in + 1 :]
-    raw, grad, turned, sent, held, core_in, load_sem, core_send, core_recv, send_sem, recv_sem = rest[:11]
-    lands = rest[11:]
+    ins, gain_ref, out_ref, gain_out, rest = refs[:n_in], refs[n_in], refs[n_in + 1], refs[n_in + 2], refs[n_in + 3 :]
+    raw, grad, turned, sent, held, core_in, gain_sum, gain_land = rest[:8]
+    load_sem, core_send, core_recv, send_sem, recv_sem, gain_send, gain_recv = rest[8:15]
+    lands = rest[15:]
+    inner = turned.shape[2] * 2
     chunks = len(sources)
     frame, group = lax.axis_index("frames"), lax.axis_index("groups")
     rows, part, places = plan.rows, plan.part, plan.places
@@ -364,15 +366,36 @@
             device_id_type=pl.DeviceIdType.MESH,
         )
 
-    def loads(t, which):
-        left, right, column = sources[which]
-        s = t % 2
-        return (
-            pltpu.make_async_copy(ins[left], raw.at[s], load_sem.at[0, s]),
+    def grad_load(t, which):
+        right, column = sources[which][1:3]
+        return pltpu.make_async_copy(
+            ins[right].at[:, column : column + CHUNK], grad.at[t % 2], load_sem.at[t % 2]
+        )
+
+    def left_start(which):
+        left, group_of = sources[which][0], sources[which][3]
+        if group_of is None:
+            pltpu.make_async_copy(ins[left], raw.at[:, 0:inner], load_sem.at[2]).start()
+            return
+        per_block = ins[left].shape[1] // plan.frames // 128
+        for block in range(plan.frames):
             pltpu.make_async_copy(
-                ins[right].at[:, column : column + CHUNK], grad.at[s], load_sem.at[1, s]
-            ),
-        )
+                ins[left].at[:, pl.ds((block * per_block + group_of) * 128, 128)],
+                raw.at[:, pl.ds(block * 128, 128)],
+                load_sem.at[3],
+            ).start()
+
+    def left_wait(which):
+        left, group_of = sources[which][0], sources[which][3]
+        width, place = (inner, 2) if group_of is None else (plan.frames * 128, 3)
+        pltpu.make_async_copy(
+            ins[left].at[:, 0:width], raw.at[:, 0:width], load_sem.at[place]
+        ).wait()
+
+    def start_loads(which, t):
+        grad_load(t, which).start()
+        if sources[which][5]:
+            left_start(which)
 
     def row_place(half):
         if halves == 1:
@@ -409,38 +432,62 @@
         held[at] = held[at] + lands[ids[i, k]][u % 2]
         step_copy(i, k + 1, u).start()
 
-    def turn(s):
-        width = 128
-        for tile in range(raw.shape[2] // width):
-            value = raw[s, :, tile * width : (tile + 1) * width].T
-            for piece in range(width // part):
-                at = tile * (width // part) + piece
-                block, half = at // halves, at % halves
-                where = xor_static(block, frame, places)
-                row = (where // 2) * rows
-                if halves > 1:
-                    row = row + xor_static(half, group, 1) * part
-                row = pl.multiple_of(row, part)
-                turned[where % 2, pl.ds(row, part), :] = value[piece * part : (piece + 1) * part, :]
+    def turn_tile(value, at):
+        for piece in range(128 // part):
+            slot, block, half = at(piece)
+            where = xor_static(block, frame, places)
+            row = (where // 2) * rows
+            if halves > 1:
+                row = row + xor_static(half, group, 1) * part
+            row = pl.multiple_of(row, part)
+            turned[slot, where % 2, pl.ds(row, part), :] = value[piece * part : (piece + 1) * part, :]
+
+    def turn(stacked):
+        for tile in range(plan.frames if stacked else inner // 128):
+            value = raw[:, tile * 128 : (tile + 1) * 128].T
+
+            def at(piece, tile=tile):
+                if stacked:
+                    return piece // halves, tile, piece % halves
+                run = tile * (128 // part) + piece
+                return 0, run // halves, run % halves
+
+            turn_tile(value, at)
+
+    def any_of(t, choices):
+        found = t == choices[0]
+        for choice in choices[1:]:
+            found = found | (t == choice)
+        return found
 
     def make(t):
         s = t % 2
-        for copy in loads(t, 0):
-            copy.wait()
+        grad_load(t, 0).wait()
+        for stacked in (True, False):
+            fresh = [w for w in range(chunks) if sources[w][5] and (sources[w][3] is not None) == stacked]
+            if fresh:
+
+                @pl.when(any_of(t, fresh))
+                def _():
+                    left_wait(fresh[0])
+                    turn(stacked)
+
         for which in range(1, chunks):
 
             @pl.when(t + 1 == which)
             def _():
-                for copy in loads(t + 1, which):
-                    copy.start()
-
-        turn(s)
+                start_loads(which, t + 1)
+
+        tslot = 0
+        for which in range(chunks):
+            if sources[which][4]:
+                tslot = jnp.where(t == which, sources[which][4], tslot)
         piece = 256
         shape = (2,) * (places - 1) + (rows, piece)
         for side in (1, 0):
             for column in range(0, CHUNK, piece):
                 value = jnp.dot(
-                    turned[side], grad[s, :, column : column + piece], preferred_element_type=WIDE
+                    turned[tslot, side], grad[s, :, column : column + piece], preferred_element_type=WIDE
                 ).astype(LOW)
                 value = value.reshape(shape)
                 at = (slice(None),) * (places - 1) + (slice(None), pl.ds(column, piece))
@@ -450,8 +497,36 @@
                     held[(t % slots,) + at] = value
         core_copy(t).start()
 
-    for copy in loads(0, 0):
-        copy.start()
+    gain_steps = [("f", d) for d in range(places)] + [("g", e) for e in range(plan.group_places)]
+
+    def gain_copy(k):
+        return pltpu.make_async_remote_copy(
+            src_ref=gain_sum,
+            dst_ref=gain_land.at[k],
+            send_sem=gain_send.at[k],
+            recv_sem=gain_recv.at[k],
+            device_id=partner(*gain_steps[k]),
+            device_id_type=pl.DeviceIdType.MESH,
+        )
+
+    def gain_work(t):
+        @pl.when(t == 0)
+        def _():
+            gain_sum[...] = gain_ref[...]
+
+        for k in range(len(gain_steps) + 1):
+
+            @pl.when(t == k + 1)
+            def _():
+                if k:
+                    gain_copy(k - 1).wait()
+                    gain_sum[...] = gain_sum[...] + gain_land[k - 1]
+                if k < len(gain_steps):
+                    gain_copy(k).start()
+                else:
+                    gain_out[...] = gain_sum[...]
+
+    start_loads(0, 0)
 
     def iteration(t, carry):
         for k in reversed(range(plan.depth)):
@@ -478,40 +553,59 @@
         def _():
             make(t)
 
+        gain_work(t)
         return carry
 
     lax.fori_loop(0, chunks + plan.depth + 1, iteration, 0)
 
 
-def reduced(pairs, frames, groups):
-    count, inner = pairs[0][0].shape
+def reduced(pairs, gains, frames, groups):
+    count = pairs[0][0].shape[0]
+    inner = min(left.shape[1] for left, _ in pairs)
     plan = Plan(frames, groups, inner)
+    per_tile = max(1, 128 // plan.rows)
     operands, sources = [], []
     for left, grad in pairs:
         at = len(operands)
         operands += [left, grad]
-        sources += [(at, at + 1, column) for column in range(0, grad.shape[1], CHUNK)]
+        stack = left.shape[1] // inner
+        if stack > 1:
+            for i in range(stack):
+                sources.append((at, at + 1, 0, i // per_tile, i % per_tile, i % per_tile == 0))
+        else:
+            for column in range(0, grad.shape[1], CHUNK):
+                sources.append((at, at + 1, column, None, 0, column == 0))
     chunks, slots = len(sources), plan.depth + 2
     half = (2,) * (plan.places - 1) + (plan.rows, CHUNK)
     steps = [step for steps in plan.steps for step in steps]
+    gain_steps = plan.places + plan.group_places
+    gain_shape = (gains.size // 128, 128)
     scratch = [
-        pltpu.VMEM((2, count, inner), LOW),
+        pltpu.VMEM((count, frames * 128), LOW),
         pltpu.VMEM((2, count, CHUNK), LOW),
-        pltpu.VMEM((2, inner // 2, count), LOW),
+        pltpu.VMEM((per_tile, 2, inner // 2, count), LOW),
         pltpu.VMEM((2,) + half, LOW),
         pltpu.VMEM((slots,) + half, LOW),
         pltpu.VMEM((2,) + half, LOW),
-        pltpu.SemaphoreType.DMA((2, 2)),
+        pltpu.VMEM(gain_shape, WIDE),
+        pltpu.VMEM((gain_steps,) + gain_shape, WIDE),
+        pltpu.SemaphoreType.DMA((4,)),
         pltpu.SemaphoreType.DMA((2,)),
         pltpu.SemaphoreType.DMA((2,)),
         pltpu.SemaphoreType.DMA((len(steps), 2)),
         pltpu.SemaphoreType.DMA((len(steps), 2)),
+        pltpu.SemaphoreType.DMA((gain_steps,)),
+        pltpu.SemaphoreType.DMA((gain_steps,)),
     ] + [pltpu.VMEM((2,) + step[-1], LOW) for step in steps]
-    result = pl.pallas_call(
+    in_vmem = pl.BlockSpec(memory_space=pltpu.VMEM)
+    result, gain_total = pl.pallas_call(
         partial(reduce_kernel, plan, sources, slots, len(operands)),
-        out_shape=jax.ShapeDtypeStruct((chunks, plan.rows, CHUNK), WIDE),
-        in_specs=[pl.BlockSpec(memory_space=pl.ANY)] * len(operands),
-        out_specs=pl.BlockSpec(memory_space=pltpu.VMEM),
+        out_shape=[
+            jax.ShapeDtypeStruct((chunks, plan.rows, CHUNK), WIDE),
+            jax.ShapeDtypeStruct(gain_shape, WIDE),
+        ],
+        in_specs=[pl.BlockSpec(memory_space=pl.ANY)] * len(operands) + [in_vmem],
+        out_specs=[in_vmem, in_vmem],
         scratch_shapes=scratch,
         compiler_params=pltpu.CompilerParams(
             collective_id=0, has_side_effects=True, vmem_limit_bytes=48 * MIB
@@ -522,13 +616,17 @@
             transcendentals=0,
         ),
         name="reduce",
-    )(*operands)
+    )(*operands, gains.reshape(gain_shape))
     outs, at = [], 0
-    for _, grad in pairs:
-        parts = grad.shape[1] // CHUNK
-        outs.append(jnp.concatenate([result[at + i] for i in range(parts)], axis=1))
-        at += parts
-    return outs
+    for left, grad in pairs:
+        stack, parts = left.shape[1] // inner, grad.shape[1] // CHUNK
+        if stack > 1:
+            outs.append(result[at : at + stack].reshape(stack * plan.rows, CHUNK))
+            at += stack
+        else:
+            outs.append(jnp.concatenate([result[at + i] for i in range(parts)], axis=1))
+            at += parts
+    return outs, gain_total.reshape(gains.shape)
 
 
 def body(
@@ -598,9 +696,6 @@
     top = (after_self + fed).astype(LOW).reshape(2, nodes, half_rows, features)
     top_latents = from_nodes(top[0], swapped(top[1], "frames", LEVEL))
 
-    grad_down = weight_grad(activated, grad_low).astype(LOW)
-    share_down = lax.psum_scatter(grad_down, "frames", scatter_dimension=0, tiled=True)
-
     grad_norm, gain_grad_mlp = norm_back(after_self, gain_mlp, grad_mlp_in)
     grad_after_self = grad_low.astype(WIDE) + grad_norm
     grad_self_out = grad_after_self.astype(LOW)
@@ -630,8 +725,10 @@
     parents_back = swapped(grad_parents[1].astype(LOW), "frames", LEVEL).astype(WIDE)
     children_back = swapped(grad_children[1].astype(LOW), "frames", LEVEL).astype(WIDE)
 
-    total_up, total_self_out, total_project, total_cross_out, total_query, total_keyval = reduced(
+    gains = jnp.stack([gain_grad_child, gain_grad_cross, gain_grad_self, gain_grad_mlp])
+    totals, gains = reduced(
         [
+            (activated, grad_low),
             (mlp_in, grad_hidden),
             (self_mixed, grad_self_out),
             (self_in, grad_projected),
@@ -639,15 +736,11 @@
             (cross_in, grad_queries),
             (child_in, grad_keyval),
         ],
+        gains,
         frames,
         groups,
     )
-    total_down = share_down
-    for place in range(groups.bit_length() - 1):
-        total_down = total_down + swapped(total_down, "groups", place)
-    total_down = total_down.astype(WIDE)
-    gains = jnp.stack([gain_grad_child, gain_grad_cross, gain_grad_self, gain_grad_mlp])
-    gains = lax.psum(gains, ("frames", "groups"))
+    total_down, total_up, total_self_out, total_project, total_cross_out, total_query, total_keyval = totals
     width = features // frames
     gains = lax.dynamic_slice_in_dim(gains, frame * width, width, 1)
     return (

time: 392 us -> 367 us (0.936)
  blocking collectives: 62.4 us -> 0 us
  Pallas kernels: 180 us -> 216 us
  waiting for transfers between devices: 17 us -> 42.4 us
  between operations: 14.9 us -> 1.66 us
  matrix products: 48.9 us -> 38.1 us
    psum x1 -> x0, blocking collectives: 62.4 us -> none  [body(): gains = lax.psum(gains, ('frames', 'groups'))]
    pallas_call x1, Pallas kernels: 124 us -> 160 us  [reduced(): pl.pallas_call(partial(reduce_kernel, plan, sources, slots, len(operands)...]
    ppermute x7 -> x6, waiting for transfers between devices: 17 us -> 42.4 us  [swapped(): lax.ppermute(value, axis, [(s, s ^ mask) for s in range(lax.axis_size(axi...]
    dot_general x1 -> x0, matrix products: 9.23 us -> none  [weight_grad(): lax.dot_general(inputs, grad_rows, (((0,), (0,)), ((), ())), preferred_el...]
    ppermute x7 -> x6, starting transfers between devices: 10.8 us -> 8.43 us  [swapped(): lax.ppermute(value, axis, [(s, s ^ mask) for s in range(lax.axis_size(axi...]
  transfers between devices with their start and end apart: 8 -> 6, of which waited for: 3 -> 4; matrix products, arithmetic and copies ran while one was open for 21% -> 12% of each run, Pallas kernels for 38% -> 3%
where the time goes in v2:
time: 367 us; the launch traced here: 362 us
  Pallas kernels  216 us (59%)
  waiting for transfers between devices  42.4 us (12%)
  matrix products  38.1 us (10%)
  other arithmetic  33.1 us (9%)
  local copies, waits for them, and re-layouts  21.4 us (6%)
  starting transfers between devices  8.43 us (2%)
    pallas_call x1, Pallas kernels, reduced(): pl.pallas_call(partial(reduce_kernel, plan, sources, slots, len(operands)...  160 us
    ppermute x6, waiting for transfers between devices, swapped(): lax.ppermute(value, axis, [(s, s ^ mask) for s in range(lax.axis_size(axi...  42.4 us
    pallas_call x1, Pallas kernels, feed(): pl.pallas_call(feed_kernel, grid=(hidden // tile,), in_specs=[whole, whol...  23.1 us
    pallas_call x2, Pallas kernels, attend_back(): pl.pallas_call(partial(attend_back_kernel, masked), grid_spec=spec, out_s...  20.6 us
    dot_general x5, matrix products, product_back(): lax.dot_general(grad_rows, weight, (((1,), (1,)), ((), ())), preferred_el...  20.1 us
    dot_general x5, matrix products, matmul(): return jnp.dot(left, right, preferred_element_type=WIDE)  17.9 us
    pallas_call x2, Pallas kernels, attend(): pl.pallas_call(partial(attend_kernel, masked), grid_spec=spec, out_shape=...  12.2 us
    ppermute x6, starting transfers between devices, swapped(): lax.ppermute(value, axis, [(s, s ^ mask) for s in range(lax.axis_size(axi...  8.43 us
  transfers between devices with their start and end apart: 6, of which 4 were waited for; matrix products, arithmetic and copies ran while one was open for 12% of the time, Pallas kernels for 3%

profile of v2, /device:TPU:0, one launch (start us, length us, event | category | flops | bytes accessed | tf_op | source)
XLA Modules:
  0.0 361.5 jit_solution(15835064877850285096)
XLA Ops:
  0.7 2.2 constant_dynamic-slice_fusion.6
  3.0 3.0 collective-permute-start
  6.0 0.9 constant_dynamic-slice_fusion.4
  7.0 1.2 constant_dynamic-slice_fusion.2
  8.1 1.9 collective-permute-start.2
  10.3 0.6 pad_add_fusion.count_ref
  10.9 8.2 %collective-permute-done = bf16[2,128,1024]{2,1,0:T(8,128)(2,1)} collective-permute-done((bf16[2,128,1024]{2,1,0:T(8,128)(2,1)}, bf16[2,128,1024]{2,1,0:T(8,128)(2,1)}, u32[]{:S(2)}, u32[]{:S(2)}) %collective-permute-start) | collective-permute-done | bytes 524320 | tf_op jit(solution)/shard_map/ppermute | solution.py:37
  19.1 1.3 convert_reduce_fusion
  20.4 1.5 fusion.2
  21.9 8.5 %collective-permute-done.1 = bf16[2,128,1024]{2,1,0:T(8,128)(2,1)} collective-permute-done((bf16[2,128,1024]{2,1,0:T(8,128)(2,1)}, bf16[2,128,1024]{2,1,0:T(8,128)(2,1)}, u32[]{:S(2)}, u32[]{:S(2)}) %collective-permute-start.1) | collective-permute-done | bytes 524320 | tf_op jit(solution)/shard_map/ppermute | solution.py:37
  30.4 1.3 convert_reduce_fusion.1
  31.6 1.5 multiply_reduce_fusion.8
  33.1 1.4 fusion.8.refs_10_
  34.6 2.2 convolution_convert_fusion.4
  36.8 1.4 multiply_convert_fusion.2.refs_12_
  38.2 3.7 %convolution_convert_fusion.1 = bf16[512,2048]{1,0:T(8,128)(2,1)} fusion(bf16[512,1024]{1,0:T(8,128)(2,1)S(1)} %multiply_convert_fusion.2.refs_12_, bf16[1024,2048]{1,0:T(8,128)(2,1)S(1)} %copy-done.33), kind=kOutput, calls=%fused_computation.1 | convolution fusion | flops 2148532224 | bytes 7340032 | tf_op jit(solution)/shard_map/dot_general | solution.py:78
  41.9 6.2 %attend.2 = bf16[2,2,128,1024]{3,2,1,0:T(8,128)(2,1)} custom-call(s32[2,2]{1,0:T(2,128)} %pad_add_fusion.count_ref, bf16[2,2,128,1024]{3,2,1,0:T(8,128)(2,1)} %bitcast.139, bf16[2,2,128,2048]{3,2,1,0:T(8,128)(2,1)} %bitcast.133, bf16[2,2,128,2048]{3,2,1,0:T(8,128)(2,1)} %bitcast.134), custom_call_target="tpu_custom_call" | custom-call | flops 536870912 | bytes 4194304 | tf_op jit(solution)/shard_map/attend/pallas_call | solution.py:171
  48.1 1.3 pad_maximum_fusion
  49.5 3.3 fusion.19
  53.2 0.9 copy-done.10
  54.5 4.9 %convolution_convert_fusion = bf16[512,3072]{1,0:T(8,128)(2,1)} fusion(bf16[512,1024]{1,0:T(8,128)(2,1)S(1)} %multiply_convert_fusion.1.refs_6_, bf16[1024,3072]{1,0:T(8,128)(2,1)S(1)} %bitcast.156), kind=kOutput, calls=%fused_computation | convolution fusion | flops 3222798336 | bytes 10485760 | tf_op jit(solution)/shard_map/dot_general | solution.py:78
  59.4 6.0 %attend.3 = bf16[2,2,128,1024]{3,2,1,0:T(8,128)(2,1)} custom-call(s32[2,2]{1,0:T(2,128)} %pad_add_fusion.count_ref, bf16[2,2,128,3072]{3,2,1,0:T(8,128)(2,1)} %bitcast.127, bf16[2,2,128,3072]{3,2,1,0:T(8,128)(2,1)} %bitcast.128, bf16[2,2,128,3072]{3,2,1,0:T(8,128)(2,1)} %bitcast.129), custom_call_target="tpu_custom_call" | custom-call | flops 536870912 | bytes 4194304 | tf_op jit(solution)/shard_map/attend/pallas_call | solution.py:171
  65.4 3.9 %fusion.20 = (f32[512]{0:T(512)S(1)}, f32[512,1024]{1,0:T(8,128)S(1)}) fusion(f32[512,1024]{1,0:T(8,128)} %copy-done.10, bf16[512,1024]{1,0:T(8,128)(2,1)} %bitcast.125, bf16[1024,1024]{1,0:T(8,128)(2,1)} %param.26), kind=kOutput, calls=%fused_computation.108 | convolution fusion | flops 1074789888 | bytes 7342080 | tf_op jit(solution)/shard_map/dot_general | solution.py:78
  70.0 0.7 copy-done.21
  70.7 1.1 pad_maximum_fusion.2
  71.8 23.1 %feed.1 = (bf16[512,4096]{1,0:T(8,128)(2,1)S(1)}, bf16[512,4096]{1,0:T(8,128)(2,1)}, f32[512,1024]{1,0:T(8,128)S(1)}, f32[512,1024]{1,0:T(8,128)S(1)}) custom-call(bf16[512,1024]{1,0:T(8,128)(2,1)S(1)} %multiply_convert_fusion.in_ref.refs_2_, bf16[512,1024]{1,0:T(8,128)(2,1)S(1)} %bitcast.123, bf16[1024,4096]{1,0:T(8,128)(2,1)} %up_ref.1, ...), custom_call_target="tpu_custom_call" | custom-call | flops 17179869184 | bytes 41943040 | tf_op jit(solution)/shard_map/feed/pallas_call | solution.py:233
  95.0 0.8 multiply_reduce_fusion
  95.8 1.2 copy-done.9
  96.9 2.4 fusion.17
  99.4 2.3 convolution_convert_fusion.3
  101.7 10.2 %attend_back.2 = bf16[2,2,128,3072]{3,2,1,0:T(8,128)(2,1)} custom-call(s32[2,2]{1,0:T(2,128)} %pad_add_fusion.count_ref, bf16[2,2,128,3072]{3,2,1,0:T(8,128)(2,1)} %bitcast.130, bf16[2,2,128,3072]{3,2,1,0:T(8,128)(2,1)} %bitcast.131, bf16[2,2,128,3072]{3,2,1,0:T(8,128)(2,1)} %bitcast.132, bf16[2,2,128,1024]{3,2,1,0:T(8,128)(2,1)} %bitcast.148), custom_call_target="tpu_custom_call" | custom-call | flops 1342177280 | bytes 7340032 | tf_op jit(solution)/shard_map/attend_back/pallas_call | solution.py:193
  111.9 8.3 %multiply_reduce_fusion.1 = (f32[1024]{0:T(1024)S(1)}, f32[512]{0:T(512)S(1)}, f32[512]{0:T(512)S(1)}, f32[512,1024]{1,0:T(8,128)S(1)}) fusion(f32[512,1024]{1,0:T(8,128)} %copy-done.10, f32[512]{0:T(512)S(1)} %add_rsqrt_fusion.1, f32[512]{0:T(512)S(1)} %broadcast_multiply_fusion.9, f32[1024]{0:T(1024)S(1)} %convert_element_type.97, ...), kind=kOutput, calls=%fused_computation.24 | convolution fusion | flops 3225417728 | bytes 13647872 | tf_op jit(solution)/shard_map/dot_general | solution.py:82
  120.2 2.0 fusion.16
  122.3 2.3 convolution_convert_fusion.2
  124.6 10.4 %attend_back.3 = (bf16[2,2,128,1024]{3,2,1,0:T(8,128)(2,1)}, bf16[2,2,128,2048]{3,2,1,0:T(8,128)(2,1)}) custom-call(s32[2,2]{1,0:T(2,128)} %pad_add_fusion.count_ref, bf16[2,2,128,1024]{3,2,1,0:T(8,128)(2,1)} %bitcast.140, bf16[2,2,128,2048]{3,2,1,0:T(8,128)(2,1)} %bitcast.135, bf16[2,2,128,2048]{3,2,1,0:T(8,128)(2,1)} %bitcast.136, ...), custom_call_target="tpu_custom_call" | custom-call | flops 1342177280 | bytes 7340032 | tf_op jit(solution)/shard_map/attend_back/pallas_call | solution.py:193
  135.0 3.4 fusion.13
  138.4 1.9 fusion.12
  140.4 0.9 slice.125
  141.2 1.0 slice.102
  142.4 3.8 %multiply_reduce_fusion.2 = (f32[1024]{0:T(1024)S(1)}, f32[512]{0:T(512)S(1)}, f32[512]{0:T(512)S(1)}, f32[512,1024]{1,0:T(8,128)S(1)}) fusion(f32[512]{0:T(512)S(1)} %rsqrt_bitcast_fusion, f32[512]{0:T(512)S(1)} %get-tuple-element.73, bf16[2,128,1024]{2,1,0:T(8,128)(2,1)} %collective-permute-done.1, bf16[2,128,1024]{2,1,0:T(8,128)(2,1)S(1)} %copy-done.15, ...), kind=kOutput, calls=%fused_computation.25 | convolution fusion | flops 2152724480 | bytes 9453568 | tf_op jit(solution)/shard_map/dot_general | solution.py:82
  146.3 1.7 subtract_multiply_fusion
  148.0 0.9 slice.124
  148.9 0.6 copy-done.18
  149.5 0.5 copy-done.3
  150.4 1.2 copy-done.7
  151.7 1.2 copy-done.8
  152.9 160.5 %reduce.9 = (f32[16,64,1024]{2,1,0:T(8,128)}, f32[32,128]{1,0:T(8,128)S(1)}) custom-call(bf16[512,4096]{1,0:T(8,128)(2,1)} %copy-done.9, bf16[512,1024]{1,0:T(8,128)(2,1)S(1)} %bitcast.124, bf16[512,1024]{1,0:T(8,128)(2,1)S(1)} %copy-done.5, bf16[512,4096]{1,0:T(8,128)(2,1)} %get-tuple-element.27.refs_3_, bf16[512,1024]{1,0:T(8,128)(2,1)S(1)} %bitcast.126, ...), custom_call_target="tpu_custom_call" | custom-call | flops 85899345920 | bytes 33554432 | tf_op jit(solution)/shard_map/reduce/pallas_call | solution.py:601
  313.4 3.0 slice_bitcast_fusion.3
  316.4 2.4 slice.99
  318.8 0.9 fusion.18
  319.7 1.5 collective-permute-start.3
  321.1 0.6 collective-permute-start.4
  321.7 1.5 collective-permute-start.5
  323.2 0.8 pad_maximum_fusion.5
  324.1 2.1 pad_maximum_fusion.3
  326.1 0.9 pad_maximum_fusion.4
  327.1 0.5 slice_bitcast_fusion.12
  327.6 18.4 %collective-permute-done.4 = bf16[2,128,1024]{2,1,0:T(8,128)(2,1)} collective-permute-done((bf16[2,128,1024]{2,1,0:T(8,128)(2,1)}, bf16[2,128,1024]{2,1,0:T(8,128)(2,1)}, u32[]{:S(2)}, u32[]{:S(2)}) %collective-permute-start.4) | collective-permute-done | bytes 524320 | tf_op jit(solution)/shard_map/ppermute | solution.py:37
  346.0 1.1 convert_element_type.109
  347.2 7.2 %collective-permute-done.5 = bf16[2,128,1024]{2,1,0:T(8,128)(2,1)} collective-permute-done((bf16[2,128,1024]{2,1,0:T(8,128)(2,1)}, bf16[2,128,1024]{2,1,0:T(8,128)(2,1)}, u32[]{:S(2)}, u32[]{:S(2)}) %collective-permute-start.5) | collective-permute-done | bytes 524320 | tf_op jit(solution)/shard_map/ppermute | solution.py:37
  354.4 1.1 convert_element_type.111
  355.6 1.6 maximum_select_fusion
  357.2 1.5 maximum_select_fusion.1
  358.7 2.4 maximum_select_fusion.2
  (107 shorter events, 2.7 us)
Async XLA Ops:
  0.6 33.9 %copy-start = (bf16[1024,1024]{1,0:T(8,128)(2,1)S(1)}, bf16[1024,1024]{1,0:T(8,128)(2,1)}, u32[]{:S(2)}) copy-start(bf16[1024,1024]{1,0:T(8,128)(2,1)} %param.21) | copy-start | bytes 6291460
  0.7 5.3 %copy-start.25 = (bf16[4,128,1024]{2,1,0:T(8,128)(2,1)S(1)}, bf16[4,128,1024]{2,1,0:T(8,128)(2,1)}, u32[]{:S(2)}) copy-start(bf16[4,128,1024]{2,1,0:T(8,128)(2,1)} %param.16) | copy-start | bytes 3145732
  0.7 6.3 %copy-start.26 = (bf16[4,128,1024]{2,1,0:T(8,128)(2,1)S(1)}, bf16[4,128,1024]{2,1,0:T(8,128)(2,1)}, u32[]{:S(2)}) copy-start(bf16[4,128,1024]{2,1,0:T(8,128)(2,1)} %param.18) | copy-start | bytes 3145732
  3.0 45.2 %copy-start.12 = (bf16[2,128,1024]{2,1,0:T(8,128)(2,1)}, bf16[2,128,1024]{2,1,0:T(8,128)(2,1)S(1)}, u32[]{:S(2)}) copy-start(bf16[2,128,1024]{2,1,0:T(8,128)(2,1)S(1)} %get-tuple-element.67) | copy-start | bytes 1572868
  3.0 7.0 %copy-start.28 = (bf16[1024]{0:T(1024)(128)(2,1)S(1)}, bf16[1024]{0:T(1024)(128)(2,1)}, u32[]{:S(2)}) copy-start(bf16[1024]{0:T(1024)(128)(2,1)} %param.20) | copy-start | bytes 6148
  3.0 7.0 %copy-start.29 = (bf16[1024]{0:T(1024)(128)(2,1)S(1)}, bf16[1024]{0:T(1024)(128)(2,1)}, u32[]{:S(2)}) copy-start(bf16[1024]{0:T(1024)(128)(2,1)} %param.19) | copy-start | bytes 6148
  3.0 7.1 %copy-start.30 = (bf16[1024]{0:T(1024)(128)(2,1)S(1)}, bf16[1024]{0:T(1024)(128)(2,1)}, u32[]{:S(2)}) copy-start(bf16[1024]{0:T(1024)(128)(2,1)} %param.24) | copy-start | bytes 6148
  3.0 7.1 %copy-start.31 = (bf16[1024]{0:T(1024)(128)(2,1)S(1)}, bf16[1024]{0:T(1024)(128)(2,1)}, u32[]{:S(2)}) copy-start(bf16[1024]{0:T(1024)(128)(2,1)} %param.27) | copy-start | bytes 6148
  3.0 7.1 %copy-start.32 = (s32[4,16]{1,0:T(4,128)S(1)}, s32[4,16]{1,0:T(4,128)}, u32[]{:S(2)}) copy-start(s32[4,16]{1,0:T(4,128)} %param.17) | copy-start | bytes 772
  3.0 16.1 %collective-permute-start = (bf16[2,128,1024]{2,1,0:T(8,128)(2,1)}, bf16[2,128,1024]{2,1,0:T(8,128)(2,1)}, u32[]{:S(2)}, u32[]{:S(2)}) collective-permute-start(bf16[2,128,1024]{2,1,0:T(8,128)(2,1)} %get-tuple-element.68), channel_id=1, source_target_pairs={{0,4},{2,6},{4,0},{6,2},{8,12},{10,14},{12,8},{14,10},{16,20},{18,... | collective-permute-start | bytes 1572872 | tf_op jit(solution)/shard_map/ppermute | solution.py:37
  6.9 29.9 %copy-start.14 = (bf16[2,128,1024]{2,1,0:T(8,128)(2,1)}, bf16[2,128,1024]{2,1,0:T(8,128)(2,1)S(1)}, u32[]{:S(2)}) copy-start(bf16[2,128,1024]{2,1,0:T(8,128)(2,1)S(1)} %get-tuple-element.65) | copy-start | bytes 1572868
  6.9 23.4 %collective-permute-start.1 = (bf16[2,128,1024]{2,1,0:T(8,128)(2,1)}, bf16[2,128,1024]{2,1,0:T(8,128)(2,1)}, u32[]{:S(2)}, u32[]{:S(2)}) collective-permute-start(bf16[2,128,1024]{2,1,0:T(8,128)(2,1)} %get-tuple-element.66), channel_id=1, source_target_pairs={{0,4},{2,6},{4,0},{6,2},{8,12},{10,14},{12,8},{14,10},{16,20},{18,... | collective-permute-start | bytes 1572872 | tf_op jit(solution)/shard_map/ppermute | solution.py:37
  8.1 61.8 %collective-permute-start.2 = (bf16[2,128,1024]{2,1,0:T(8,128)(2,1)}, bf16[2,128,1024]{2,1,0:T(8,128)(2,1)}, u32[]{:S(2)}, u32[]{:S(2)}) collective-permute-start(bf16[2,128,1024]{2,1,0:T(8,128)(2,1)} %get-tuple-element.64), channel_id=1, source_target_pairs={{0,4},{2,6},{4,0},{6,2},{8,12},{10,14},{12,8},{14,10},{16,20},{18,... | collective-permute-start | bytes 1572872 | tf_op jit(solution)/shard_map/ppermute | solution.py:37
  34.5 2.3 copy-start.23
  34.5 3.7 %copy-start.33 = (bf16[1024,2048]{1,0:T(8,128)(2,1)S(1)}, bf16[1024,2048]{1,0:T(8,128)(2,1)}, u32[]{:S(2)}) copy-start(bf16[1024,2048]{1,0:T(8,128)(2,1)} %param.22) | copy-start | bytes 12582916
  38.2 3.7 %copy-start.24 = (bf16[512,1024]{1,0:T(8,128)(2,1)}, bf16[512,1024]{1,0:T(8,128)(2,1)S(1)}, u32[]{:S(2)}) copy-start(bf16[512,1024]{1,0:T(8,128)(2,1)S(1)} %multiply_convert_fusion.2.refs_12_) | copy-start | bytes 3145732
  48.1 1.4 copy-start.27
  48.1 6.3 %slice-start.1 = ((s8[6291456]{0:T(1024)(128)(4,1)}), s8[4194304]{0:T(1024)(128)(4,1)S(1)}, s32[]{:S(2)}) async-start(s8[6291456]{0:T(1024)(128)(4,1)} %bitcast.155), calls=%async_computation.1 | async-start | bytes 8388608
  49.5 5.0 %slice-start.2 = ((s8[6291456]{0:T(1024)(128)(4,1)}), s8[2097152]{0:T(1024)(128)(4,1)S(1)}, s32[]{:S(2)}) async-start(s8[6291456]{0:T(1024)(128)(4,1)} %bitcast.155), calls=%async_computation.2 | async-start | bytes 4194304
  52.8 1.3 copy-start.10
  54.5 4.9 %copy-start.2 = (bf16[512,1024]{1,0:T(8,128)(2,1)}, bf16[512,1024]{1,0:T(8,128)(2,1)S(1)}, u32[]{:S(2)}) copy-start(bf16[512,1024]{1,0:T(8,128)(2,1)S(1)} %multiply_convert_fusion.1.refs_6_) | copy-start | bytes 3145732
  69.6 1.0 copy-start.21
  70.0 25.0 %copy-start.4 = (bf16[512,1024]{1,0:T(8,128)(2,1)}, bf16[512,1024]{1,0:T(8,128)(2,1)S(1)}, u32[]{:S(2)}) copy-start(bf16[512,1024]{1,0:T(8,128)(2,1)S(1)} %multiply_convert_fusion.in_ref.refs_2_) | copy-start | bytes 3145732
  95.0 2.0 copy-start.9
  96.9 2.4 copy-start.35
  99.4 2.3 copy-start.6
  111.9 8.3 %copy-start.11 = (f32[512,1024]{1,0:T(8,128)S(1)}, f32[512,1024]{1,0:T(8,128)}, u32[]{:S(2)}) copy-start(f32[512,1024]{1,0:T(8,128)} %copy-done.10) | copy-start | bytes 6291460
  111.9 8.3 %copy-start.17 = (f32[512,1024]{1,0:T(8,128)S(1)}, f32[512,1024]{1,0:T(8,128)}, u32[]{:S(2)}) copy-start(f32[512,1024]{1,0:T(8,128)} %get-tuple-element.47) | copy-start | bytes 6291460
  120.2 2.0 copy-start.36
  122.3 2.3 copy-start.22
  135.0 3.4 copy-start.13
  135.0 3.4 copy-start.16
  138.4 3.8 %copy-start.34 = (bf16[1024,2048]{1,0:T(8,128)(2,1)S(1)}, bf16[1024,2048]{1,0:T(8,128)(2,1)}, u32[]{:S(2)}) copy-start(bf16[1024,2048]{1,0:T(8,128)(2,1)} %param.22) | copy-start | bytes 12582916
  140.3 1.9 copy-start.15
  140.4 2.0 copy-start.37
  147.9 1.5 copy-start.18
  148.0 2.0 copy-start.3
  148.0 2.5 copy-start.5
  150.4 1.2 copy-start.7
  151.7 1.2 copy-start.8
  316.4 2.4 copy-start.19
  319.7 39.1 %collective-permute-start.3 = (bf16[2,128,1024]{2,1,0:T(8,128)(2,1)}, bf16[2,128,1024]{2,1,0:T(8,128)(2,1)}, u32[]{:S(2)}, u32[]{:S(2)}) collective-permute-start(bf16[2,128,1024]{2,1,0:T(8,128)(2,1)} %bitcast.13), channel_id=1, source_target_pairs={{0,4},{2,6},{4,0},{6,2},{8,12},{10,14},{12,8},{14,10},{16,20},{18,... | collective-permute-start | bytes 1572872 | tf_op jit(solution)/shard_map/ppermute | solution.py:37
  321.1 24.9 %collective-permute-start.4 = (bf16[2,128,1024]{2,1,0:T(8,128)(2,1)}, bf16[2,128,1024]{2,1,0:T(8,128)(2,1)}, u32[]{:S(2)}, u32[]{:S(2)}) collective-permute-start(bf16[2,128,1024]{2,1,0:T(8,128)(2,1)} %bitcast.19), channel_id=1, source_target_pairs={{0,4},{2,6},{4,0},{6,2},{8,12},{10,14},{12,8},{14,10},{16,20},{18,... | collective-permute-start | bytes 1572872 | tf_op jit(solution)/shard_map/ppermute | solution.py:37
  321.7 32.7 %collective-permute-start.5 = (bf16[2,128,1024]{2,1,0:T(8,128)(2,1)}, bf16[2,128,1024]{2,1,0:T(8,128)(2,1)}, u32[]{:S(2)}, u32[]{:S(2)}) collective-permute-start(bf16[2,128,1024]{2,1,0:T(8,128)(2,1)} %bitcast.22), channel_id=1, source_target_pairs={{0,4},{2,6},{4,0},{6,2},{8,12},{10,14},{12,8},{14,10},{16,20},{18,... | collective-permute-start | bytes 1572872 | tf_op jit(solution)/shard_map/ppermute | solution.py:37
  326.1 29.4 %copy-start.20 = (f32[256,1024]{1,0:T(8,128)S(1)}, f32[256,1024]{1,0:T(8,128)}, u32[]{:S(2)}) copy-start(f32[256,1024]{1,0:T(8,128)} %slice.102) | copy-start | bytes 3145732
  355.6 1.6 slice-start
  357.2 3.9 %copy-start.1 = (bf16[1024,1024]{1,0:T(8,128)(2,1)S(1)}, bf16[1024,1024]{1,0:T(8,128)(2,1)}, u32[]{:S(2)}) copy-start(bf16[1024,1024]{1,0:T(8,128)(2,1)} %param.21) | copy-start | bytes 6291460
